TPU v7x, 512 devices: a whole 4x4x16 slice. The times are simulated.
512 devices in a mesh: dp: 64 (over z, y), tensor: 8 (over x, core).
Axes of the slice: x: 4, y: 4, z: 16, core: 2. Of those that a mesh axis runs over, the one named last changes fastest.
Arguments:
- layer_input: bfloat16 [8192, 8192], P('dp', 'tensor'), may hold values from -6 to 6
- output_grad: bfloat16 [8192, 8192], P('dp', 'tensor'), may hold values from -0.06591797 to 0.06591797
- gate_pre: bfloat16 [8192, 28672], P('dp', 'tensor'), may hold values from -6 to 6
- up_pre: bfloat16 [8192, 28672], P('dp', 'tensor'), may hold values from -6 to 6
- hidden_grad: bfloat16 [8192, 28672], P('dp', 'tensor'), may hold values from -0.06591797 to 0.06591797
- tile_list: int32 [448, 3], P('tensor'), may hold values from 0 to 63, as said below
- tile_slots: int32 [448], P('tensor'), may hold values from 0 to 127, as said below
- first_codes: int32 [8, 128, 16384], P('tensor', 'dp'), may hold values from 0 to 255
- second_codes: int32 [8, 128, 16384], P('tensor', 'dp'), may hold values from 0 to 255
- first_absmax: float32 [8, 128, 8], P('tensor', 'dp'), may hold values from 0.05 to 0.5
- second_absmax: float32 [8, 128, 8], P('tensor', 'dp'), may hold values from 0.005 to 0.05
- signed_map: float32 [256], replicated, may hold values from -1 to 1
- unsigned_map: float32 [256], replicated, may hold values from 0.05 to 1
Outputs:
- update_tiles: bfloat16 [448, 128, 128], P('tensor')
- first_moment: float32 [8, 128, 16384], P('tensor', 'dp')
- second_moment: float32 [8, 128, 16384], P('tensor', 'dp')
Inputs may be any that keep to these rules, and one draw needn't show every extreme that they name: `tile_list`: within each group of 56 rows that belongs to one tensor index the triples are distinct; the first entry is below 64, the second below 28, the third is 0, 1 or 2. `tile_slots`: within each group of 56 entries the slots are distinct; a dp index owns slots s with s // 2 equal to it, so it holds at most 2 tiles of a group, and in every group some dp index holds exactly 2.
All inputs are finite; a program needn't handle non-finite values.
Results may differ from a plain program's by a relative error of at most 0.0085.
Values may be sent and summed in bfloat16 or wider, within the bound.
A program may use at most 64 MiB of HBM per device.

v0:
```python
import jax
import jax.numpy as jnp
from jax import lax
from jax.sharding import PartitionSpec as P

CAP = 2
TB = 128
STEP = 10


BETA_FIRST = 0.9
BETA_SECOND = 0.99
EPSILON = 1e-08


def lookup(code_table, level_table):
    levels = jnp.arange(16, dtype=jnp.int32)
    high_part = jnp.right_shift(code_table, 4)
    low_part = jnp.bitwise_and(code_table, 15)
    low_onehot = (low_part[:, None, :] == levels[None, :, None]).astype(jnp.bfloat16)
    high_onehot = (high_part[:, None, :] == levels[None, :, None]).astype(jnp.float32)
    square = level_table.reshape(16, 16)
    first_part = square.astype(jnp.bfloat16)
    remain = square - first_part.astype(jnp.float32)
    second_part = remain.astype(jnp.bfloat16)
    third_part = (remain - second_part.astype(jnp.float32)).astype(jnp.bfloat16)
    total = jnp.zeros(code_table.shape, jnp.float32)
    for level_part in (third_part, second_part, first_part):
        by_high = jnp.einsum(
            "hl,cln->chn", level_part, low_onehot, preferred_element_type=jnp.float32
        )
        total = total + jnp.sum(by_high * high_onehot, axis=1)
    return total


def dequantize(code_table, level_table, scales):
    values = lookup(code_table, level_table)
    shaped = values.reshape(code_table.shape[0], scales.shape[1], -1) * scales[:, :, None]
    return shaped.reshape(code_table.shape)


def body(
    layer_input,
    output_grad,
    gate_pre,
    up_pre,
    hidden_grad,
    tile_list,
    tile_slots,
    first_codes,
    second_codes,
    first_absmax,
    second_absmax,
    signed_map,
    unsigned_map,
):
    whole_input, whole_grad = (
        lax.all_gather(layer_input, "tensor", axis=1, tiled=True),
        lax.all_gather(output_grad, "tensor", axis=1, tiled=True),
    )
    tokens_here = whole_input.shape[0]
    tile_count = tile_list.shape[0]
    gate_value = gate_pre.astype(jnp.float32)
    up_value = up_pre.astype(jnp.float32)
    grad_value = hidden_grad.astype(jnp.float32)
    sigmoid_gate = jax.nn.sigmoid(gate_value)
    silu_gate = gate_value * sigmoid_gate
    hidden = (silu_gate * up_value).astype(jnp.bfloat16)
    gate_grad = (
        grad_value * up_value * sigmoid_gate * (1.0 + gate_value * (1.0 - sigmoid_gate))
    ).astype(jnp.bfloat16)
    up_grad = (grad_value * silu_gate).astype(jnp.bfloat16)
    width_block = tile_list[:, 0]
    hidden_block = tile_list[:, 1]
    matrix_id = tile_list[:, 2][None, :, None]

    def blocks(source, block_index):
        return jnp.take(source.reshape(tokens_here, -1, TB), block_index, axis=1)

    left_side = jnp.where(
        matrix_id == 2, blocks(hidden, hidden_block), blocks(whole_input, width_block)
    )
    right_side = jnp.where(
        matrix_id == 0,
        blocks(gate_grad, hidden_block),
        jnp.where(matrix_id == 1, blocks(up_grad, hidden_block), blocks(whole_grad, width_block)),
    )
    partial_value = jnp.einsum(
        "tki,tkj->kij", left_side, right_side, preferred_element_type=jnp.float32
    )
    partial_value = partial_value.reshape(tile_count, -1)
    owner_index = lax.axis_index("dp")
    slot_ids = owner_index * CAP + jnp.arange(CAP, dtype=jnp.int32)
    summed = lax.psum(partial_value, "dp")
    slot_match = (tile_slots[None, :] == slot_ids[:, None]).astype(jnp.float32)
    own_grad = jnp.dot(slot_match, summed, precision=lax.Precision.HIGHEST)
    first_old = dequantize(first_codes[0], signed_map, first_absmax[0])
    second_old = dequantize(second_codes[0], unsigned_map, second_absmax[0])
    first_moment = BETA_FIRST * first_old + (1.0 - BETA_FIRST) * own_grad
    second_moment = BETA_SECOND * second_old + (1.0 - BETA_SECOND) * own_grad * own_grad
    first_hat = first_moment / (1.0 - BETA_FIRST**STEP)
    second_hat = second_moment / (1.0 - BETA_SECOND**STEP)
    slot_update = (first_hat / (jnp.sqrt(second_hat) + EPSILON)).astype(jnp.bfloat16)
    everyone = lax.all_gather(slot_update, "dp", axis=0, tiled=True)
    picked = jnp.take(everyone, tile_slots, axis=0)
    return (picked.reshape(tile_count, TB, TB), first_moment[None], second_moment[None])


def solution(mesh):
    in_specs = (
        P("dp", "tensor"),
        P("dp", "tensor"),
        P("dp", "tensor"),
        P("dp", "tensor"),
        P("dp", "tensor"),
        P("tensor", None),
        P("tensor"),
        P("tensor", "dp", None),
        P("tensor", "dp", None),
        P("tensor", "dp", None),
        P("tensor", "dp", None),
        P(),
        P(),
    )
    out_specs = (P("tensor", None, None), P("tensor", "dp", None), P("tensor", "dp", None))
    return jax.shard_map(body, mesh=mesh, in_specs=in_specs, out_specs=out_specs, check_vma=False)
```

profile of v0, /device:TPU:6, one launch (start us, length us, event | category | flops | bytes accessed | tf_op | source)
XLA Modules:
  0.0 557.6 jit_solution(2680922352320135020)
XLA Ops:
  7.2 0.0 copy-start
  7.2 0.0 copy-start.2
  7.2 0.0 all-gather.7.cloned.1.call-start
  7.2 1.9 copy.42
  9.2 0.0 all-gather.7.cloned.1.call-update
  9.2 0.0 all-gather.5.cloned.1.call-start
  9.2 1.8 copy.37
  11.0 0.0 all-gather.5.cloned.1.call-update
  11.0 0.0 all-reduce.2.cloned.1.call-start
  11.1 0.8 compare_and_fusion.1
  11.9 0.6 copy.34
  12.5 0.0 copy-start.4
  12.5 1.3 copy.35
  13.8 1.3 copy.39
  15.1 3.5 fusion.6
  18.6 0.6 copy.36
  19.2 1.6 copy.40
  20.8 2.2 gather_fusion.1
  23.0 2.0 gather_fusion.3
  25.0 0.6 copy.41
  25.7 0.0 copy-start.8
  25.7 0.0 copy-start.9
  25.7 0.0 copy-start.7
  25.7 0.0 copy-start.5
  25.7 2.1 gather_fusion.4
  27.8 0.0 copy-done.8
  27.8 0.1 reshape.126
  27.9 0.0 copy-done.9
  27.9 0.1 reshape.133
  27.9 0.0 copy-done
  27.9 0.1 broadcast_bitcast_fusion.1
  28.0 0.1 copy.46
  28.1 0.1 broadcast_bitcast_fusion
  28.2 0.1 copy.48
  28.4 0.1 shift-right-arithmetic_bitcast_fusion
  28.5 0.9 fusion.36
  29.4 0.7 compare_bitcast_fusion.2
  30.0 16.3 %all-gather.7.cloned.1.call-done = bf16[128,8192]{0,1:T(8,128)(2,1)} async-done(((bf16[128,1024]{0,1:T(8,128)(2,1)}), bf16[128,8192]{0,1:T(8,128)(2,1)}) %all-gather.7.cloned.1.call-update) | async-done | bytes 2097168 | tf_op jit(solution)/shard_map/all_gather | solution.py:59
  46.4 3.2 copy.43
  49.6 32.4 %all-gather.5.cloned.1.call-done = bf16[128,8192]{0,1:T(8,128)(2,1)} async-done(((bf16[128,1024]{0,1:T(8,128)(2,1)}), bf16[128,8192]{0,1:T(8,128)(2,1)}) %all-gather.5.cloned.1.call-update) | async-done | bytes 2097168 | tf_op jit(solution)/shard_map/all_gather | solution.py:58
  82.0 4.1 copy.38
  86.0 2.0 gather_fusion.5
  88.1 3.8 gather_fusion.2
  91.8 4.2 fusion.16
  96.0 3.9 copy.51
  99.9 0.0 all-reduce.2.cloned.1.call-update
  100.0 0.2 all-gather.9.cloned.1.call-start
  100.2 0.6 copy-done.6
  100.8 0.1 shift-right-arithmetic_bitcast_fusion.1
  100.9 0.9 fusion.33
  101.8 0.9 fusion.32
  102.7 0.9 fusion.35
  103.6 0.9 fusion.31
  104.5 0.0 copy-start.10
  104.5 0.9 fusion.34
  105.4 284.1 %all-reduce.2.cloned.1.call-done = f32[56,16384]{1,0:T(8,128)} async-done(((f32[56,16384]{1,0:T(8,128)}), f32[56,16384]{1,0:T(8,128)}) %all-reduce.2.cloned.1.call-update) | async-done | bytes 3670032 | tf_op jit(solution)/shard_map/psum | solution.py:94
  389.6 0.0 copy-done.10
  389.6 4.4 fusion.46
  394.0 0.0 all-gather.9.cloned.1.call-update
  394.1 141.6 %all-gather.9.cloned.1.call-done = bf16[64,2,16384]{2,1,0:T(2,128)(2,1)} async-done(((bf16[1,2,16384]{2,1,0:T(2,128)(2,1)}), bf16[64,2,16384]{2,1,0:T(2,128)(2,1)}) %all-gather.9.cloned.1.call-update) | async-done | bytes 4194320 | tf_op jit(solution)/shard_map/all_gather | solution.py:104
  535.7 7.2 %reshape.189 = bf16[128,16384]{1,0:T(8,128)(2,1)} reshape(bf16[64,2,16384]{2,1,0:T(2,128)(2,1)} %all-gather.9.cloned.1.call-done) | data formatting | bytes 8388608
  542.9 6.0 %gather_fusion = bf16[56,16384]{1,0:T(8,128)(2,1)S(1)} fusion(bf16[128,16384]{1,0:T(8,128)(2,1)} %reshape.189, s32[1024]{0:T(1024)S(1)} %pad_clamp_fusion), kind=kCustom, calls=%fused_computation.5 | custom fusion | bytes 3670240 | tf_op jit(solution)/shard_map/jit(_take)/gather | solution.py:105
  549.0 0.5 copy.49
  549.5 1.6 bitcast_select_fusion
  (14 shorter events, 0.0 us)
Async XLA Ops:
  7.2 20.8 %copy-start = (f32[1,2,8]{2,1,0:T(2,128)S(1)}, f32[1,2,8]{2,1,0:T(2,128)}, u32[]{:S(2)}) copy-start(f32[1,2,8]{2,1,0:T(2,128)} %param.26) | copy-start | bytes 196
  7.2 4.7 copy-start.2
  7.2 5.3 copy-start.3
  7.2 39.2 %all-gather.7.cloned.1.call-start = ((), (), s32[]{:S(2)}) async-start(), calls=%async_computation.1 | async-start | bytes 2359296 | tf_op jit(solution)/shard_map/all_gather | solution.py:59
  9.2 72.8 %all-gather.5.cloned.1.call-start = ((), (), s32[]{:S(2)}) async-start(), calls=%async_computation | async-start | bytes 2359296 | tf_op jit(solution)/shard_map/all_gather | solution.py:58
  11.0 378.5 %all-reduce.2.cloned.1.call-start = ((), (), s32[]{:S(2)}) async-start(), calls=%async_computation.2 | async-start | bytes 7340032 | tf_op jit(solution)/shard_map/psum | solution.py:94
  12.5 1.3 copy-start.4
  25.7 2.1 copy-start.8
  25.7 2.2 copy-start.9
  25.7 2.4 copy-start.7
  25.7 2.6 copy-start.5
  88.1 3.8 copy-start.1
  99.9 0.9 copy-start.6
  100.0 435.7 %all-gather.9.cloned.1.call-start = ((), (), s32[]{:S(2)}) async-start(), calls=%async_computation.3 | async-start | bytes 4259840 | tf_op jit(solution)/shard_map/all_gather | solution.py:104
  104.5 285.0 %copy-start.10 = (s32[56]{0:T(128)S(1)}, s32[56]{0:T(128)}, u32[]{:S(2)}) copy-start(s32[56]{0:T(128)} %param.23) | copy-start | bytes 676
Sparse Core Ops, SparseCore 0:
  10.2 36.1 all-gather.6
  48.5 33.4 all-gather.4
  100.1 289.4 all-reduce.1
  394.2 141.4 all-gather.8
where the time goes:
time: 558 us
  waiting for transfers between devices  475 us (85%)
  local copies, waits for them, and re-layouts  47.9 us (9%)
  matrix products  14 us (3%)
  between operations  14 us (3%)
  other arithmetic  6.76 us (1%)
    psum x1, waiting for transfers between devices, body(): summed = lax.psum(partial_value, 'dp')  284 us
    all_gather x1, waiting for transfers between devices, body(): everyone = lax.all_gather(slot_update, 'dp', axis=0, tiled=True)  142 us
    all_gather x1, waiting for transfers between devices, body(): lax.all_gather(layer_input, 'tensor', axis=1, tiled=True)  32.4 us
    unnamed x34, local copies, waits for them, and re-layouts  19.6 us
    all_gather x1, waiting for transfers between devices, body(): lax.all_gather(output_grad, 'tensor', axis=1, tiled=True)  16.3 us
    gather x5, local copies, waits for them, and re-layouts, blocks(): return jnp.take(source.reshape(tokens_here, -1, TB), block_index, axis=1)  12.1 us
  transfers between devices with their start and end apart: 4, of which 4 were waited for; matrix products, arithmetic and copies ran while one was open for 5% of the time, Pallas kernels for 0%

commit v1 on v0

v1 whole, which is shorter than its diff:
```python
import functools

import jax
import jax.numpy as jnp
from jax import lax
from jax.experimental import pallas as pl
from jax.experimental.pallas import tpu as pltpu
from jax.sharding import PartitionSpec as P

CAP = 2
TB = 128
QB = 2048
STEP = 10
BETA_FIRST = 0.9
BETA_SECOND = 0.99
EPSILON = 1e-08

NX, NY, NZ = 4, 4, 16
TILES = 56
WB = 64
HB = 28
OWN = WB // 8
ROWS = TILES * TB // (NY * NZ)
HALF = NZ // 2
MESH = pl.DeviceIdType.MESH
F32, BF16 = jnp.float32, jnp.bfloat16


def up_to(value, size):
    return lax.rem(value, size)


class Place:
    def __init__(self):
        dp, t = lax.axis_index("dp"), lax.axis_index("tensor")
        self.dp, self.t = dp, t
        self.z, self.y = dp // NY, lax.rem(dp, NY)
        self.x, self.c = t // 2, lax.rem(t, 2)

    def along_x(self, d):
        return (self.dp, up_to(self.x + NX + d, NX) * 2 + self.c)

    def partner(self):
        return (self.dp, self.x * 2 + 1 - self.c)

    def along_y(self, d):
        return (self.z * NY + up_to(self.y + NY + d, NY), self.t)

    def along_z(self, d):
        return (up_to(self.z + NZ + d, NZ) * NY + self.y, self.t)


def remote(src, dst, send, recv, device):
    return pltpu.make_async_remote_copy(
        src_ref=src, dst_ref=dst, send_sem=send, recv_sem=recv, device_id=device, device_id_type=MESH
    )


class Gather:
    def __init__(self, place, left, right, send, recv):
        self.place, self.left, self.right, self.send, self.recv = place, left, right, send, recv
        self.sent = []

    def piece(self, d, other, p):
        pc = self.place
        core = 1 - pc.c if other else pc.c
        owner = up_to(pc.x + NX + d, NX) * 2 + core
        if p < 2:
            return self.right.at[pl.ds(2 * HB + owner * OWN + p * 4, 4)]
        return self.left.at[pl.ds(owner * OWN + (p - 2) * 4, 4)]

    def copy(self, route, p):
        pc = self.place
        shift = {0: 0, 1: 0, 2: 0, 3: -1, 4: 1, 5: -1 if p % 2 == 0 else 1, 6: 2}[route]
        to = {0: pc.along_x(1), 1: pc.along_x(-1), 5: pc.along_x(1 if p % 2 == 0 else -1)}.get(route)
        to = pc.partner() if to is None else to
        block = self.piece(shift, False, p)
        return remote(block, block, self.send.at[route, p], self.recv.at[route, p], to)

    def start(self, route, p):
        one = self.copy(route, p)
        one.start()
        self.sent.append(one)

    def arrived(self, route, p):
        shift, other = {
            0: (-1, False),
            1: (1, False),
            2: (0, True),
            3: (-1, True),
            4: (1, True),
            5: (2, False),
            6: (2, True),
        }[route]
        block = self.piece(shift, other, p)
        remote(
            block, block, self.send.at[route, p], self.recv.at[route, p], self.place.partner()
        ).wait_recv()

    def begin(self, p):
        for route in (0, 1, 2):
            self.start(route, p)

    def step(self, i):
        if i < 4:
            self.arrived(0, i)
            if i % 2 == 0:
                self.start(5, i)
            self.start(3, i)
            self.arrived(1, i)
            if i % 2 == 1:
                self.start(5, i)
            self.start(4, i)
        elif i < 8:
            self.arrived(5, i - 4)
            self.start(6, i - 4)

    def finish(self):
        for p in range(4):
            for route in (2, 3, 4, 6):
                self.arrived(route, p)
        for one in self.sent:
            one.wait_send()


class Scatter:
    def __init__(self, place, source, bufs, send, recv, kept):
        self.place, self.source, self.send, self.recv, self.kept = place, source, send, recv, kept
        self.s1, self.r1, self.s2, self.r2, self.sz, self.rz = bufs
        self.sent = []

    def own(self, zz, dy):
        yy = up_to(self.place.y + NY + dy, NY)
        start = pl.multiple_of((zz * NY + yy) * ROWS, 16)
        return self.source[:, pl.ds(start, ROWS), :]

    def zs(self, j):
        z = self.place.z
        return up_to(z + HALF - j, NZ), up_to(z + NZ - (HALF - 1 - j), NZ)

    def copy(self, kind, d, j):
        src, dst = ((self.s1, self.r1), (self.s2, self.r2), (self.sz, self.rz))[kind]
        way = 1 if d == 0 else -1
        to = self.place.along_z(way) if kind == 2 else self.place.along_y(way)
        return remote(src.at[d, j], dst.at[d, j], self.send.at[kind, d, j], self.recv.at[kind, d, j], to)

    def start(self, kind, d, j):
        one = self.copy(kind, d, j)
        one.start()
        self.sent.append(one)

    def first(self, j):
        za, zb = self.zs(j)
        self.s1[0, j] = self.own(za, 2)
        self.start(0, 0, j)
        self.s1[1, j] = self.own(zb, 2)
        self.start(0, 1, j)

    def second(self, j):
        za, zb = self.zs(j)
        self.s2[0, j, 1] = self.own(zb, 1)
        self.s2[1, j, 0] = self.own(za, -1)
        self.copy(0, 0, j).wait_recv()
        self.s2[0, j, 0] = (self.r1[0, j].astype(F32) + self.own(za, 1).astype(F32)).astype(BF16)
        self.start(1, 0, j)
        self.copy(0, 1, j).wait_recv()
        self.s2[1, j, 1] = (self.r1[1, j].astype(F32) + self.own(zb, -1).astype(F32)).astype(BF16)
        self.start(1, 1, j)

    def third(self, j):
        za, zb = self.zs(j)
        self.copy(1, 0, j).wait_recv()
        self.copy(1, 1, j).wait_recv()
        sum_a = self.own(za, 0).astype(F32) + self.r2[0, j, 0].astype(F32) + self.r2[1, j, 0].astype(F32)
        sum_b = self.own(zb, 0).astype(F32) + self.r2[0, j, 1].astype(F32) + self.r2[1, j, 1].astype(F32)
        if j > 0:
            self.copy(2, 0, j - 1).wait_recv()
            sum_a = sum_a + self.rz[0, j - 1].astype(F32)
        self.sz[0, j] = sum_a.astype(BF16)
        self.start(2, 0, j)
        if j > 0:
            self.copy(2, 1, j - 1).wait_recv()
            sum_b = sum_b + self.rz[1, j - 1].astype(F32)
        if j < HALF - 1:
            self.sz[1, j] = sum_b.astype(BF16)
            self.start(2, 1, j)
        else:
            self.kept[...] = sum_b

    def slot(self, i):
        if i < HALF:
            self.first(i)
        if 0 <= i - 1 < HALF:
            self.second(i - 1)
        if 0 <= i - 2 < HALF:
            self.third(i - 2)

    def finish(self):
        self.copy(2, 0, HALF - 1).wait_recv()
        self.kept[...] = self.kept[...] + self.rz[0, HALF - 1].astype(F32)
        for one in self.sent:
            one.wait_send()


class Spread:
    def __init__(self, place, rows, zsend, zrecv, ysend, yrecv, give):
        self.place, self.rows, self.give = place, rows, give
        self.zsend, self.zrecv, self.ysend, self.yrecv = zsend, zrecv, ysend, yrecv
        self.sent = []

    def zq(self, q):
        z = self.place.z
        if q == 0:
            return z
        if q % 2 == 1:
            return up_to(z + NZ - 1 - (q - 1) // 2, NZ)
        return up_to(z + 1 + (q - 2) // 2, NZ)

    def at(self, zz, dy):
        return zz * NY + up_to(self.place.y + NY + dy, NY)

    def zcopy(self, d, j, received):
        z = self.place.z
        back = j + 1 if received else j
        zz = up_to(z + NZ - back, NZ) if d == 0 else up_to(z + back, NZ)
        ref = self.rows.at[self.at(zz, 0)]
        to = self.place.along_z(1 if d == 0 else -1)
        return remote(ref, ref, self.zsend.at[d, j], self.zrecv.at[d, j], to)

    def ycopy(self, hop, d, q, received):
        way = 1 if d == 0 else -1
        dy = -way * (hop + 1) if received else -way * hop
        ref = self.rows.at[self.at(self.zq(q), dy)]
        if hop == 1:
            ref = ref.at[d]
        to = self.place.along_y(way)
        return remote(ref, ref, self.ysend.at[hop, d, q], self.yrecv.at[hop, d, q], to)

    def start(self, one):
        one.start()
        self.sent.append(one)

    def out_y(self, q):
        self.start(self.ycopy(0, 0, q, False))
        self.start(self.ycopy(0, 1, q, False))

    def on_y(self, q):
        self.ycopy(0, 0, q, True).wait_recv()
        self.start(self.ycopy(1, 0, q, False))
        self.ycopy(0, 1, q, True).wait_recv()
        self.start(self.ycopy(1, 1, q, False))

    def done(self, q):
        self.ycopy(1, 0, q, True).wait_recv()
        self.ycopy(1, 1, q, True).wait_recv()
        zz = self.zq(q)
        for dy in range(NY):
            self.give(self.at(zz, dy))

    def run(self):
        self.start(self.zcopy(0, 0, False))
        self.start(self.zcopy(1, 0, False))
        self.out_y(0)
        groups = [[0]]
        for j in range(HALF + 4):
            if j < HALF:
                group = [1 + 2 * j]
                self.zcopy(0, j, True).wait_recv()
                if j < HALF - 1:
                    self.start(self.zcopy(0, j + 1, False))
                    self.zcopy(1, j, True).wait_recv()
                    if j < HALF - 2:
                        self.start(self.zcopy(1, j + 1, False))
                    group.append(2 + 2 * j)
                for q in group:
                    self.out_y(q)
                groups.append(group)
            if j < len(groups):
                for q in groups[j]:
                    self.on_y(q)
            if 0 <= j - 2 < len(groups):
                for q in groups[j - 2]:
                    self.done(q)
        for one in self.sent:
            one.wait_send()


def dequantize(fscale, sscale, fcodes, scodes, smap, umap, exact, rounded):
    for a, (codes, table, scale) in enumerate(((fcodes, smap, fscale), (scodes, umap, sscale))):
        low_table = jnp.broadcast_to(table[0:1, :], (16, TB))
        high_table = jnp.broadcast_to(table[1:2, :], (16, TB))
        for s in range(CAP):
            for b in range(TB * TB // QB):
                block = slice(b * 16, (b + 1) * 16)
                code = codes[s, block, :]
                low = jnp.bitwise_and(code, TB - 1)
                value = jnp.where(
                    code < TB,
                    jnp.take_along_axis(low_table, low, axis=1, mode="promise_in_bounds"),
                    jnp.take_along_axis(high_table, low, axis=1, mode="promise_in_bounds"),
                )
                value = value * scale[s, b]
                exact[a, s, block, :] = value
                rounded[a, s, block, :] = value.astype(BF16)
        rounded[a, CAP] = jnp.zeros((TB, TB), BF16)


def kernel(
    list_ref,
    slots_ref,
    exact_ref,
    rounded_ref,
    input_ref,
    grad_ref,
    gate_ref,
    up_ref,
    hgrad_ref,
    update_ref,
    first_ref,
    second_ref,
    left,
    right,
    parts,
    states,
    rows,
    summed,
    old_kept,
    sum_kept,
    e1,
    f1,
    e2,
    f2,
    ez,
    fz,
    p1,
    q1,
    p2,
    q2,
    pz,
    qz,
    gsend,
    grecv,
    esend,
    erecv,
    psend,
    precv,
    zsend,
    zrecv,
    ysend,
    yrecv,
):
    place = Place()
    barrier = pltpu.get_barrier_semaphore()
    near = [place.partner()]
    for d in (1, -1):
        near += [place.along_x(d), place.along_y(d), place.along_z(d)]
    for device in near:
        pl.semaphore_signal(barrier, inc=1, device_id=device, device_id_type=MESH)

    gather = Gather(place, left, right, gsend, grecv)
    for j in range(OWN):
        right[2 * HB + place.t * OWN + j] = grad_ref[:, j * TB : (j + 1) * TB]
    pl.semaphore_wait(barrier, len(near))
    gather.begin(0)
    gather.begin(1)
    for j in range(OWN):
        left[place.t * OWN + j] = input_ref[:, j * TB : (j + 1) * TB].T
    gather.begin(2)
    gather.begin(3)

    def fill(k, carry):
        slot = slots_ref[k]
        mine = jnp.where(lax.shift_right_logical(slot, 1) == place.dp, jnp.bitwise_and(slot, 1), CAP)
        for a in range(2):
            states[a, pl.ds(pl.multiple_of(k * TB, TB), TB), :] = rounded_ref[a, mine]
        return carry

    lax.fori_loop(0, TILES, fill, 0)

    def activations(i):
        for h in range(4 * i, 4 * i + 4):
            cols = slice(h * TB, (h + 1) * TB)
            gate = gate_ref[:, cols].astype(F32)
            up = up_ref[:, cols].astype(F32)
            grad = hgrad_ref[:, cols].astype(F32)
            sigmoid = 1.0 / (1.0 + jnp.exp(-gate))
            silu = gate * sigmoid
            left[WB + h] = (silu * up).astype(BF16).T
            right[h] = (grad * up * sigmoid * (1.0 + gate * (1.0 - sigmoid))).astype(BF16)
            right[HB + h] = (grad * silu).astype(BF16)

    olds = Scatter(place, states, (e1, f1, e2, f2, ez, fz), esend, erecv, old_kept)
    for i in range(HALF + 2):
        olds.slot(i)
        gather.step(i)
        if i < HB // 4:
            activations(i)
    olds.finish()
    gather.finish()

    def multiply(k, carry):
        width, hidden, matrix = list_ref[k, 0], list_ref[k, 1], list_ref[k, 2]
        li = jnp.where(matrix == 2, WB + hidden, width)
        ri = jnp.where(matrix == 2, 2 * HB + width, jnp.where(matrix == 1, HB + hidden, hidden))
        tile = jnp.dot(left[li], right[ri], preferred_element_type=F32)
        parts[0, pl.ds(pl.multiple_of(k * TB, TB), TB), :] = tile.astype(BF16)
        return carry

    lax.fori_loop(0, TILES, multiply, 0, unroll=4)

    sums = Scatter(place, parts, (p1, q1, p2, q2, pz, qz), psend, precv, sum_kept)
    for i in range(HALF + 2):
        sums.slot(i)
    sums.finish()

    def moments(first_old, second_old, grad):
        first = BETA_FIRST * first_old + (1.0 - BETA_FIRST) * grad
        second = BETA_SECOND * second_old + (1.0 - BETA_SECOND) * grad * grad
        return first, second

    grad = sum_kept[0]
    first, second = moments(old_kept[0], old_kept[1], grad)
    first_hat = first / (1.0 - BETA_FIRST**STEP)
    second_hat = second / (1.0 - BETA_SECOND**STEP)
    rows[place.dp, 0] = (first_hat / (jnp.sqrt(second_hat) + EPSILON)).astype(BF16)
    rows[place.dp, 1] = grad.astype(BF16)

    def give(dp):
        where = pl.ds(pl.multiple_of(dp * ROWS, 16), ROWS)
        update_ref[where, :] = rows[dp, 0]
        summed[pl.ds(dp * (ROWS // 16), ROWS // 16)] = rows[dp, 1].reshape(ROWS // 16, 16, TB)

    summed[pl.ds(TILES * 8, 8)] = jnp.zeros((8, 16, TB), BF16)
    Spread(place, rows, zsend, zrecv, ysend, yrecv, give).run()

    for s in range(CAP):
        mine = place.dp * CAP + s
        k = lax.fori_loop(
            0, TILES, lambda i, found: jnp.where(slots_ref[i] == mine, i, found), jnp.int32(TILES)
        )
        for b in range(8):
            block = slice(b * 16, (b + 1) * 16)
            grad = summed[k * 8 + b].astype(F32)
            first, second = moments(exact_ref[0, s, block, :], exact_ref[1, s, block, :], grad)
            first_ref[s, block, :] = first
            second_ref[s, block, :] = second


def body(
    layer_input,
    output_grad,
    gate_pre,
    up_pre,
    hidden_grad,
    tile_list,
    tile_slots,
    first_codes,
    second_codes,
    first_absmax,
    second_absmax,
    signed_map,
    unsigned_map,
):
    vmem = pl.BlockSpec(memory_space=pltpu.VMEM)
    smem = pl.BlockSpec(memory_space=pltpu.SMEM)

    def scatter_shapes(n):
        one = [pltpu.VMEM((2, HALF, n, ROWS, TB), BF16)] * 2
        two = [pltpu.VMEM((2, HALF, 2, n, ROWS, TB), BF16)] * 2
        return one + two + one

    exact, rounded = pl.pallas_call(
        dequantize,
        out_shape=(
            jax.ShapeDtypeStruct((2, CAP, TB, TB), F32),
            jax.ShapeDtypeStruct((2, CAP + 1, TB, TB), BF16),
        ),
        in_specs=[smem] * 2 + [vmem] * 4,
        out_specs=[vmem] * 2,
    )(
        first_absmax[0],
        second_absmax[0],
        first_codes.reshape(CAP, TB, TB),
        second_codes.reshape(CAP, TB, TB),
        signed_map.reshape(2, TB),
        unsigned_map.reshape(2, TB),
    )
    dma = pltpu.SemaphoreType.DMA
    update, first, second = pl.pallas_call(
        kernel,
        out_shape=(
            jax.ShapeDtypeStruct((TILES * TB, TB), BF16),
            jax.ShapeDtypeStruct((CAP, TB, TB), F32),
            jax.ShapeDtypeStruct((CAP, TB, TB), F32),
        ),
        in_specs=[smem] * 2 + [vmem] * 7,
        out_specs=[vmem] * 3,
        scratch_shapes=[
            pltpu.VMEM((WB + HB, TB, TB), BF16),
            pltpu.VMEM((WB + 2 * HB, TB, TB), BF16),
            pltpu.VMEM((1, TILES * TB, TB), BF16),
            pltpu.VMEM((2, TILES * TB, TB), BF16),
            pltpu.VMEM((NY * NZ, 2, ROWS, TB), BF16),
            pltpu.VMEM(((TILES + 1) * 8, 16, TB), BF16),
            pltpu.VMEM((2, ROWS, TB), F32),
            pltpu.VMEM((1, ROWS, TB), F32),
        ]
        + scatter_shapes(2)
        + scatter_shapes(1)
        + [dma((7, 4))] * 2
        + [dma((3, 2, HALF))] * 4
        + [dma((2, HALF))] * 2
        + [dma((2, 2, NZ))] * 2,
        compiler_params=pltpu.CompilerParams(
            collective_id=0, has_side_effects=True, vmem_limit_bytes=60 * 1024 * 1024
        ),
    )(
        tile_list,
        tile_slots,
        exact,
        rounded,
        layer_input,
        output_grad,
        gate_pre,
        up_pre,
        hidden_grad,
    )
    return (
        update.reshape(TILES, TB, TB),
        first.reshape(1, CAP, TB * TB),
        second.reshape(1, CAP, TB * TB),
    )


def solution(mesh):
    in_specs = (
        P("dp", "tensor"),
        P("dp", "tensor"),
        P("dp", "tensor"),
        P("dp", "tensor"),
        P("dp", "tensor"),
        P("tensor", None),
        P("tensor"),
        P("tensor", "dp", None),
        P("tensor", "dp", None),
        P("tensor", "dp", None),
        P("tensor", "dp", None),
        P(),
        P(),
    )
    out_specs = (P("tensor", None, None), P("tensor", "dp", None), P("tensor", "dp", None))
    return jax.shard_map(body, mesh=mesh, in_specs=in_specs, out_specs=out_specs, check_vma=False)
```

time: 558 us -> 144 us (0.26)
  waiting for transfers between devices: 475 us -> 0 us
  Pallas kernels: 0 us -> 132 us
  local copies, waits for them, and re-layouts: 47.9 us -> 9.28 us
  matrix products: 14 us -> 0 us
  between operations: 14 us -> 0.64 us
  other arithmetic: 6.76 us -> 0 us
    psum x1 -> x0, waiting for transfers between devices: 284 us -> none  [body(): summed = lax.psum(partial_value, 'dp')]
    all_gather x3 -> x0, waiting for transfers between devices: 190 us -> none  [the longest x1 142 us: body(): everyone = lax.all_gather(slot_update, 'dp', axis=0, tiled=True)]
    pallas_call x0 -> x2, Pallas kernels: none -> 132 us  [the longest x1 130 us: body(): pl.pallas_call(kernel, out_shape=(jax.ShapeDtypeStruct((TILES * TB, TB),...]
    gather x6 -> x0, local copies, waits for them, and re-layouts: 18.1 us -> none  [the longest x5 12.1 us: blocks(): return jnp.take(source.reshape(tokens_here, -1, TB), block_index, axis=1)]
    unnamed x34 -> x2, local copies, waits for them, and re-layouts: 19.6 us -> 4.32 us
    dot_general x8 -> x0, matrix products: 14 us -> none  [the longest x6 5.39 us: lookup(): jnp.einsum('hl,cln->chn', level_part, low_onehot, preferred_element_type=...]
  transfers between devices with their start and end apart: 4 -> 0, of which waited for: 4 -> 0; matrix products, arithmetic and copies ran while one was open for 5% -> 0% of each run, Pallas kernels for 0% -> 0%
where the time goes in v1:
time: 144 us; the launch traced here: 142 us
  Pallas kernels  132 us (92%)
  local copies, waits for them, and re-layouts  9.28 us (6%)
    pallas_call x1, Pallas kernels, body(): pl.pallas_call(kernel, out_shape=(jax.ShapeDtypeStruct((TILES * TB, TB),...  130 us
    unnamed x2, local copies, waits for them, and re-layouts  4.32 us

profile of v1, /device:TPU:6, one launch (start us, length us, event | category | flops | bytes accessed | tf_op | source)
XLA Modules:
  0.0 141.9 jit_solution(4093694629329419396)
XLA Ops:
  0.6 1.4 copy.16.list_ref
  2.0 1.7 %copy_bitcast_fusion = (s32[2,128,128]{2,1,0:T(8,128)}, s32[2,128,128]{2,1,0:T(8,128)}) fusion(s32[1,2,128,128]{3,1,2,0:T(2,128)} %bitcast.14, s32[1,2,128,128]{3,1,2,0:T(2,128)} %bitcast.15), kind=kLoop, calls=%fused_computation | loop fusion | bytes 524288 | tf_op jit(solution)/shard_map/reshape | solution.py:484
  3.7 2.1 %shard_map.148 = (f32[2,2,128,128]{3,2,1,0:T(8,128)}, bf16[2,3,128,128]{3,2,1,0:T(8,128)(2,1)}) custom-call(f32[2,8]{1,0:T(2,128)} %bitcast.16, f32[2,8]{1,0:T(2,128)} %bitcast.17, s32[2,128,128]{2,1,0:T(8,128)} %get-tuple-element.14.fcodes, s32[2,128,128]{2,1,0:T(8,128)} %get-tuple-element.13.scodes, f32[2,128]{1,0:T(2,128)} %bitcast.18, f32[2,128]{1,0:T(2,128)} %bitcast.19), custom_call_target="tpu_custom_call" | custom-call | tf_op jit(solution)/shard_map/pallas_call | solution.py:472
  5.8 129.8 %shard_map.149 = (bf16[7168,128]{1,0:T(8,128)(2,1)}, f32[2,128,128]{2,1,0:T(8,128)}, f32[2,128,128]{2,1,0:T(8,128)}) custom-call(s32[56,3]{1,0:T(8,128)} %copy.16.list_ref, s32[56]{0:T(128)} %slots_ref.1, f32[2,2,128,128]{3,2,1,0:T(8,128)} %get-tuple-element.8.exact_ref, bf16[2,3,128,128]{3,2,1,0:T(8,128)(2,1)} %get-tuple-element.9.rounded_ref, ...), custom_call_target="tpu_custom_call" | custom-call | tf_op jit(solution)/shard_map/pallas_call | solution.py:489
  135.7 1.6 %reshape.32 = f32[1,2,16384]{2,1,0:T(2,128)} reshape(f32[2,128,128]{2,1,0:T(8,128)} %get-tuple-element.11) | data formatting | bytes 262144 | tf_op jit(solution)/shard_map/reshape | solution.py:530
  137.3 1.6 %reshape.33 = f32[1,2,16384]{2,1,0:T(2,128)} reshape(f32[2,128,128]{2,1,0:T(8,128)} %get-tuple-element.12) | data formatting | bytes 262144 | tf_op jit(solution)/shard_map/reshape | solution.py:531
  138.9 2.9 %copy.22 = bf16[56,128,128]{2,1,0:T(8,128)(2,1)} copy(bf16[56,128,128]{2,1,0:T(8,128)(2,1)} %bitcast.13) | data formatting | bytes 3670016

commit v2 on v1

--- a/solution.py
+++ b/solution.py
@@ -22,6 +22,7 @@
 OWN = WB // 8
 ROWS = TILES * TB // (NY * NZ)
 HALF = NZ // 2
+LAG = 2
 MESH = pl.DeviceIdType.MESH
 F32, BF16 = jnp.float32, jnp.bfloat16
 
@@ -190,10 +191,10 @@
     def slot(self, i):
         if i < HALF:
             self.first(i)
-        if 0 <= i - 1 < HALF:
-            self.second(i - 1)
-        if 0 <= i - 2 < HALF:
-            self.third(i - 2)
+        if 0 <= i - LAG < HALF:
+            self.second(i - LAG)
+        if 0 <= i - 2 * LAG < HALF:
+            self.third(i - 2 * LAG)
 
     def finish(self):
         self.copy(2, 0, HALF - 1).wait_recv()
@@ -202,9 +203,73 @@
             one.wait_send()
 
 
+class Pool:
+    def __init__(self, place, pool, send, recv):
+        self.place, self.pool, self.send, self.recv = place, pool, send, recv
+        self.sent = []
+
+    def copy(self, hop, d, received):
+        way = 1 if d == 0 else -1
+        back = -way * (hop + 1) if received else -way * hop
+        yy = up_to(self.place.y + NY + back, NY)
+        ref = self.pool.at[pl.ds(yy * CAP, CAP)] if hop == 0 else self.pool.at[yy * CAP + d]
+        return remote(ref, ref, self.send.at[hop, d], self.recv.at[hop, d], self.place.along_y(way))
+
+    def start(self, hop):
+        for d in range(2):
+            if hop == 1:
+                self.copy(0, d, True).wait_recv()
+            one = self.copy(hop, d, False)
+            one.start()
+            self.sent.append(one)
+
+    def finish(self):
+        for d in range(2):
+            self.copy(1, d, True).wait_recv()
+        for one in self.sent:
+            one.wait_send()
+
+
+class Olds:
+    def __init__(self, place, states, out, into, send, recv, kept):
+        self.place, self.states, self.out, self.into = place, states, out, into
+        self.send, self.recv, self.kept = send, recv, kept
+        self.sent = []
+
+    def copy(self, d, j):
+        to = self.place.along_z(1 if d == 0 else -1)
+        return remote(self.out.at[d, j], self.into.at[d, j], self.send.at[d, j], self.recv.at[d, j], to)
+
+    def own(self, zz):
+        start = pl.multiple_of((zz * NY + self.place.y) * ROWS, 16)
+        return self.states[:, pl.ds(start, ROWS), :].astype(F32)
+
+    def slot(self, j):
+        z = self.place.z
+        far = (up_to(z + HALF - j, NZ), up_to(z + NZ - (HALF - 1 - j), NZ))
+        for d in range(2):
+            value = self.own(far[d])
+            if j > 0:
+                self.copy(d, j - 1).wait_recv()
+                value = value + self.into[d, j - 1].astype(F32)
+            if d == 1 and j == HALF - 1:
+                self.kept[...] = value
+            else:
+                self.out[d, j] = value.astype(BF16)
+                one = self.copy(d, j)
+                one.start()
+                self.sent.append(one)
+
+    def finish(self):
+        self.copy(0, HALF - 1).wait_recv()
+        self.kept[...] = self.kept[...] + self.into[0, HALF - 1].astype(F32)
+        for one in self.sent:
+            one.wait_send()
+
+
 class Spread:
-    def __init__(self, place, rows, zsend, zrecv, ysend, yrecv, give):
-        self.place, self.rows, self.give = place, rows, give
+    def __init__(self, place, rows, zsend, zrecv, ysend, yrecv, give, take):
+        self.place, self.rows, self.give, self.take = place, rows, give, take
         self.zsend, self.zrecv, self.ysend, self.yrecv = zsend, zrecv, ysend, yrecv
         self.sent = []
 
@@ -219,20 +284,20 @@
     def at(self, zz, dy):
         return zz * NY + up_to(self.place.y + NY + dy, NY)
 
-    def zcopy(self, d, j, received):
+    def zcopy(self, what, d, j, received):
         z = self.place.z
         back = j + 1 if received else j
         zz = up_to(z + NZ - back, NZ) if d == 0 else up_to(z + back, NZ)
-        ref = self.rows.at[self.at(zz, 0)]
+        ref = self.rows.at[self.at(zz, 0), what]
         to = self.place.along_z(1 if d == 0 else -1)
-        return remote(ref, ref, self.zsend.at[d, j], self.zrecv.at[d, j], to)
+        return remote(ref, ref, self.zsend.at[what, d, j], self.zrecv.at[what, d, j], to)
 
     def ycopy(self, hop, d, q, received):
         way = 1 if d == 0 else -1
         dy = -way * (hop + 1) if received else -way * hop
-        ref = self.rows.at[self.at(self.zq(q), dy)]
+        ref = self.rows.at[self.at(self.zq(q), dy), 0]
         if hop == 1:
-            ref = ref.at[d]
+            ref = ref.at[pl.ds(0, 64)] if d == 0 else ref.at[pl.ds(64, ROWS - 64)]
         to = self.place.along_y(way)
         return remote(ref, ref, self.ysend.at[hop, d, q], self.yrecv.at[hop, d, q], to)
 
@@ -257,32 +322,100 @@
         for dy in range(NY):
             self.give(self.at(zz, dy))
 
-    def run(self):
-        self.start(self.zcopy(0, 0, False))
-        self.start(self.zcopy(1, 0, False))
+    def hops(self, j):
+        return (0, 1) if j < HALF - 1 else (0,)
+
+    def along_z(self, what, j):
+        for d in self.hops(j):
+            self.zcopy(what, d, j, True).wait_recv()
+            if d in self.hops(j + 1) and j + 1 < HALF:
+                self.start(self.zcopy(what, d, j + 1, False))
+        return [1 + 2 * j + d for d in self.hops(j)]
+
+    def begin(self, what):
+        for d in range(2):
+            self.start(self.zcopy(what, d, 0, False))
+
+    def run(self, collect):
+        self.begin(0)
+        self.begin(1)
         self.out_y(0)
+        self.take(self.at(self.place.z, 0))
         groups = [[0]]
         for j in range(HALF + 4):
             if j < HALF:
-                group = [1 + 2 * j]
-                self.zcopy(0, j, True).wait_recv()
-                if j < HALF - 1:
-                    self.start(self.zcopy(0, j + 1, False))
-                    self.zcopy(1, j, True).wait_recv()
-                    if j < HALF - 2:
-                        self.start(self.zcopy(1, j + 1, False))
-                    group.append(2 + 2 * j)
+                group = self.along_z(0, j)
                 for q in group:
                     self.out_y(q)
                 groups.append(group)
+            if 0 < j <= HALF:
+                for q in self.along_z(1, j - 1):
+                    self.take(self.at(self.zq(q), 0))
+            if j == HALF:
+                collect.first()
             if j < len(groups):
                 for q in groups[j]:
                     self.on_y(q)
+            if j == HALF + 1:
+                collect.second()
             if 0 <= j - 2 < len(groups):
                 for q in groups[j - 2]:
                     self.done(q)
         for one in self.sent:
             one.wait_send()
+
+
+class Collect:
+    def __init__(self, place, tiles, summed, out, into, relay, last, send, recv):
+        self.place, self.tiles, self.summed = place, tiles, summed
+        self.out, self.into, self.relay, self.last = out, into, relay, last
+        self.send, self.recv = send, recv
+        self.sent = []
+
+    def copy(self, hop, d):
+        src, dst = (
+            (self.out.at[d], self.into.at[d]),
+            (self.out.at[2, d], self.relay.at[d]),
+            (self.relay.at[d], self.last.at[d]),
+        )[hop]
+        to = self.place.along_y(1 if d == 0 else -1)
+        return remote(src, dst, self.send.at[hop, d], self.recv.at[hop, d], to)
+
+    def start(self, hop, d):
+        one = self.copy(hop, d)
+        one.start()
+        self.sent.append(one)
+
+    def first(self):
+        for n in (2, 0, 1):
+            for s in range(CAP):
+                k = self.tiles[n * CAP + s]
+                for b in range(8):
+                    self.out[n, s, b * 16 : (b + 1) * 16, :] = self.summed[k * 8 + b]
+            if n == 2:
+                self.start(1, 0)
+                self.start(1, 1)
+            else:
+                self.start(0, n)
+
+    def second(self):
+        for d in range(2):
+            self.copy(1, d).wait_recv()
+            self.start(2, d)
+
+    def finish(self):
+        for hop in (0, 2):
+            for d in range(2):
+                self.copy(hop, d).wait_recv()
+        for one in self.sent:
+            one.wait_send()
+
+    def grad(self, s, b):
+        block = slice(b * 16, (b + 1) * 16)
+        value = self.summed[self.tiles[3 * CAP + s] * 8 + b].astype(F32)
+        for other in (self.into[0, s, block, :], self.into[1, s, block, :], self.last[s, block, :]):
+            value = value + other.astype(F32)
+        return value
 
 
 def dequantize(fscale, sscale, fcodes, scodes, smap, umap, exact, rounded):
@@ -301,8 +434,7 @@
                 )
                 value = value * scale[s, b]
                 exact[a, s, block, :] = value
-                rounded[a, s, block, :] = value.astype(BF16)
-        rounded[a, CAP] = jnp.zeros((TB, TB), BF16)
+                rounded[s, a, block, :] = value.astype(BF16)
 
 
 def kernel(
@@ -322,24 +454,27 @@
     right,
     parts,
     states,
+    pool,
     rows,
     summed,
     old_kept,
     sum_kept,
-    e1,
-    f1,
-    e2,
-    f2,
-    ez,
-    fz,
+    oz,
+    iz,
     p1,
     q1,
     p2,
     q2,
     pz,
     qz,
+    cout,
+    cinto,
+    crelay,
+    clast,
     gsend,
     grecv,
+    osend,
+    orecv,
     esend,
     erecv,
     psend,
@@ -348,6 +483,8 @@
     zrecv,
     ysend,
     yrecv,
+    csend,
+    crecv,
 ):
     place = Place()
     barrier = pltpu.get_barrier_semaphore()
@@ -357,25 +494,20 @@
     for device in near:
         pl.semaphore_signal(barrier, inc=1, device_id=device, device_id_type=MESH)
 
+    shared = Pool(place, pool, osend, orecv)
+    pool[pl.ds(place.y * CAP, CAP)] = rounded_ref[...]
+    pool[NY * CAP] = jnp.zeros((2, TB, TB), BF16)
     gather = Gather(place, left, right, gsend, grecv)
     for j in range(OWN):
         right[2 * HB + place.t * OWN + j] = grad_ref[:, j * TB : (j + 1) * TB]
     pl.semaphore_wait(barrier, len(near))
+    shared.start(0)
     gather.begin(0)
     gather.begin(1)
     for j in range(OWN):
         left[place.t * OWN + j] = input_ref[:, j * TB : (j + 1) * TB].T
     gather.begin(2)
     gather.begin(3)
-
-    def fill(k, carry):
-        slot = slots_ref[k]
-        mine = jnp.where(lax.shift_right_logical(slot, 1) == place.dp, jnp.bitwise_and(slot, 1), CAP)
-        for a in range(2):
-            states[a, pl.ds(pl.multiple_of(k * TB, TB), TB), :] = rounded_ref[a, mine]
-        return carry
-
-    lax.fori_loop(0, TILES, fill, 0)
 
     def activations(i):
         for h in range(4 * i, 4 * i + 4):
@@ -389,17 +521,41 @@
             right[h] = (grad * up * sigmoid * (1.0 + gate * (1.0 - sigmoid))).astype(BF16)
             right[HB + h] = (grad * silu).astype(BF16)
 
-    olds = Scatter(place, states, (e1, f1, e2, f2, ez, fz), esend, erecv, old_kept)
-    for i in range(HALF + 2):
+    def fill(k, carry):
+        slot = slots_ref[k]
+        near = lax.shift_right_logical(slot, 3) == place.z
+        mine = jnp.where(near, jnp.bitwise_and(slot, NY * CAP - 1), NY * CAP)
+        for a in range(2):
+            states[a, pl.ds(pl.multiple_of(k * TB, TB), TB), :] = pool[mine, a]
+        return carry
+
+    olds = Olds(place, states, oz, iz, esend, erecv, old_kept)
+    activations(0)
+    shared.start(1)
+    activations(1)
+    gather.step(0)
+    shared.finish()
+    lax.fori_loop(0, TILES, fill, 0)
+    for i in range(HALF):
         olds.slot(i)
-        gather.step(i)
-        if i < HB // 4:
-            activations(i)
+        gather.step(i + 1)
+        if i + 2 < HB // 4:
+            activations(i + 2)
+
+    def find(k, found):
+        slot = slots_ref[k]
+        return tuple(jnp.where(slot == one, k, old) for one, old in zip(wanted, found))
+
+    wanted = [
+        (place.z * NY + up_to(place.y + NY + dy, NY)) * CAP + s for dy in (1, -1, 2, 0) for s in range(CAP)
+    ]
+    tiles = lax.fori_loop(0, TILES, find, (jnp.int32(TILES),) * len(wanted))
+    summed[...] = jnp.zeros(summed.shape, BF16)
     olds.finish()
     gather.finish()
 
     def multiply(k, carry):
-        width, hidden, matrix = list_ref[k, 0], list_ref[k, 1], list_ref[k, 2]
+        width, hidden, matrix = list_ref[0, k], list_ref[1, k], list_ref[2, k]
         li = jnp.where(matrix == 2, WB + hidden, width)
         ri = jnp.where(matrix == 2, 2 * HB + width, jnp.where(matrix == 1, HB + hidden, hidden))
         tile = jnp.dot(left[li], right[ri], preferred_element_type=F32)
@@ -409,7 +565,7 @@
     lax.fori_loop(0, TILES, multiply, 0, unroll=4)
 
     sums = Scatter(place, parts, (p1, q1, p2, q2, pz, qz), psend, precv, sum_kept)
-    for i in range(HALF + 2):
+    for i in range(HALF + 2 * LAG):
         sums.slot(i)
     sums.finish()
 
@@ -426,21 +582,18 @@
     rows[place.dp, 1] = grad.astype(BF16)
 
     def give(dp):
-        where = pl.ds(pl.multiple_of(dp * ROWS, 16), ROWS)
-        update_ref[where, :] = rows[dp, 0]
+        update_ref[pl.ds(pl.multiple_of(dp * ROWS, 16), ROWS), :] = rows[dp, 0]
+
+    def take(dp):
         summed[pl.ds(dp * (ROWS // 16), ROWS // 16)] = rows[dp, 1].reshape(ROWS // 16, 16, TB)
 
-    summed[pl.ds(TILES * 8, 8)] = jnp.zeros((8, 16, TB), BF16)
-    Spread(place, rows, zsend, zrecv, ysend, yrecv, give).run()
-
+    collect = Collect(place, tiles, summed, cout, cinto, crelay, clast, csend, crecv)
+    Spread(place, rows, zsend, zrecv, ysend, yrecv, give, take).run(collect)
+    collect.finish()
     for s in range(CAP):
-        mine = place.dp * CAP + s
-        k = lax.fori_loop(
-            0, TILES, lambda i, found: jnp.where(slots_ref[i] == mine, i, found), jnp.int32(TILES)
-        )
         for b in range(8):
             block = slice(b * 16, (b + 1) * 16)
-            grad = summed[k * 8 + b].astype(F32)
+            grad = collect.grad(s, b)
             first, second = moments(exact_ref[0, s, block, :], exact_ref[1, s, block, :], grad)
             first_ref[s, block, :] = first
             second_ref[s, block, :] = second
@@ -473,7 +626,7 @@
         dequantize,
         out_shape=(
             jax.ShapeDtypeStruct((2, CAP, TB, TB), F32),
-            jax.ShapeDtypeStruct((2, CAP + 1, TB, TB), BF16),
+            jax.ShapeDtypeStruct((CAP, 2, TB, TB), BF16),
         ),
         in_specs=[smem] * 2 + [vmem] * 4,
         out_specs=[vmem] * 2,
@@ -500,22 +653,32 @@
             pltpu.VMEM((WB + 2 * HB, TB, TB), BF16),
             pltpu.VMEM((1, TILES * TB, TB), BF16),
             pltpu.VMEM((2, TILES * TB, TB), BF16),
+            pltpu.VMEM((NY * CAP + 1, 2, TB, TB), BF16),
             pltpu.VMEM((NY * NZ, 2, ROWS, TB), BF16),
             pltpu.VMEM(((TILES + 1) * 8, 16, TB), BF16),
             pltpu.VMEM((2, ROWS, TB), F32),
             pltpu.VMEM((1, ROWS, TB), F32),
         ]
-        + scatter_shapes(2)
+        + [pltpu.VMEM((2, HALF, 2, ROWS, TB), BF16)] * 2
         + scatter_shapes(1)
+        + [
+            pltpu.VMEM((3, CAP, TB, TB), BF16),
+            pltpu.VMEM((2, CAP, TB, TB), BF16),
+            pltpu.VMEM((2, TB, TB), BF16),
+            pltpu.VMEM((2, TB, TB), BF16),
+        ]
         + [dma((7, 4))] * 2
-        + [dma((3, 2, HALF))] * 4
+        + [dma((2, 2))] * 2
         + [dma((2, HALF))] * 2
-        + [dma((2, 2, NZ))] * 2,
+        + [dma((3, 2, HALF))] * 2
+        + [dma((2, 2, HALF))] * 2
+        + [dma((2, 2, NZ))] * 2
+        + [dma((3, 2))] * 2,
         compiler_params=pltpu.CompilerParams(
             collective_id=0, has_side_effects=True, vmem_limit_bytes=60 * 1024 * 1024
         ),
     )(
-        tile_list,
+        tile_list.T,
         tile_slots,
         exact,
         rounded,

time: 144 us -> 138 us (0.958)
  the two profiles are of different devices: /device:TPU:6 before, /device:TPU:8 now
where the time goes in v2:
time: 138 us
  Pallas kernels  129 us (93%)
  local copies, waits for them, and re-layouts  7.9 us (6%)
    pallas_call x1, Pallas kernels, body(): pl.pallas_call(kernel, out_shape=(jax.ShapeDtypeStruct((TILES * TB, TB),...  127 us
    unnamed x1, local copies, waits for them, and re-layouts  2.94 us

profile of v2, /device:TPU:8, one launch (start us, length us, event | category | flops | bytes accessed | tf_op | source)
XLA Modules:
  0.0 137.8 jit_solution(297089471268846766)
XLA Ops:
  0.6 1.7 %copy_bitcast_fusion = (s32[2,128,128]{2,1,0:T(8,128)}, s32[2,128,128]{2,1,0:T(8,128)}) fusion(s32[1,2,128,128]{3,1,2,0:T(2,128)} %bitcast.15, s32[1,2,128,128]{3,1,2,0:T(2,128)} %bitcast.16), kind=kLoop, calls=%fused_computation | loop fusion | bytes 524288 | tf_op jit(solution)/shard_map/reshape | solution.py:637
  2.3 2.1 %shard_map.148 = (f32[2,2,128,128]{3,2,1,0:T(8,128)}, bf16[2,2,128,128]{3,2,1,0:T(8,128)(2,1)}) custom-call(f32[2,8]{1,0:T(2,128)} %bitcast.18, f32[2,8]{1,0:T(2,128)} %bitcast.19, s32[2,128,128]{2,1,0:T(8,128)} %get-tuple-element.14.fcodes, s32[2,128,128]{2,1,0:T(8,128)} %get-tuple-element.13.scodes, f32[2,128]{1,0:T(2,128)} %bitcast.20, f32[2,128]{1,0:T(2,128)} %bitcast.21), custom_call_target="tpu_custom_call" | custom-call | tf_op jit(solution)/shard_map/pallas_call | solution.py:625
  4.4 127.2 %shard_map.149 = (bf16[7168,128]{1,0:T(8,128)(2,1)}, f32[2,128,128]{2,1,0:T(8,128)}, f32[2,128,128]{2,1,0:T(8,128)}) custom-call(s32[3,56]{1,0:T(4,128)} %bitcast.17, s32[56]{0:T(128)} %slots_ref.1, f32[2,2,128,128]{3,2,1,0:T(8,128)} %get-tuple-element.8.exact_ref, bf16[2,2,128,128]{3,2,1,0:T(8,128)(2,1)} %get-tuple-element.9.rounded_ref, ...), custom_call_target="tpu_custom_call" | custom-call | tf_op jit(solution)/shard_map/pallas_call | solution.py:642
  131.6 1.6 %reshape.32 = f32[1,2,16384]{2,1,0:T(2,128)} reshape(f32[2,128,128]{2,1,0:T(8,128)} %get-tuple-element.11) | data formatting | bytes 262144 | tf_op jit(solution)/shard_map/reshape | solution.py:693
  133.2 1.6 %reshape.33 = f32[1,2,16384]{2,1,0:T(2,128)} reshape(f32[2,128,128]{2,1,0:T(8,128)} %get-tuple-element.12) | data formatting | bytes 262144 | tf_op jit(solution)/shard_map/reshape | solution.py:694
  134.9 2.9 %copy.21 = bf16[56,128,128]{2,1,0:T(8,128)(2,1)} copy(bf16[56,128,128]{2,1,0:T(8,128)(2,1)} %bitcast.14) | data formatting | bytes 3670016

commit v3 on v2

--- a/solution.py
+++ b/solution.py
@@ -55,6 +55,10 @@
     return pltpu.make_async_remote_copy(
         src_ref=src, dst_ref=dst, send_sem=send, recv_sem=recv, device_id=device, device_id_type=MESH
     )
+
+
+def leap(d, j):
+    return min(2, HALF - d - j)
 
 
 class Gather:
@@ -142,7 +146,7 @@
     def copy(self, kind, d, j):
         src, dst = ((self.s1, self.r1), (self.s2, self.r2), (self.sz, self.rz))[kind]
         way = 1 if d == 0 else -1
-        to = self.place.along_z(way) if kind == 2 else self.place.along_y(way)
+        to = self.place.along_z(way * leap(d, j)) if kind == 2 else self.place.along_y(way)
         return remote(src.at[d, j], dst.at[d, j], self.send.at[kind, d, j], self.recv.at[kind, d, j], to)
 
     def start(self, kind, d, j):
@@ -174,14 +178,14 @@
         self.copy(1, 1, j).wait_recv()
         sum_a = self.own(za, 0).astype(F32) + self.r2[0, j, 0].astype(F32) + self.r2[1, j, 0].astype(F32)
         sum_b = self.own(zb, 0).astype(F32) + self.r2[0, j, 1].astype(F32) + self.r2[1, j, 1].astype(F32)
-        if j > 0:
-            self.copy(2, 0, j - 1).wait_recv()
-            sum_a = sum_a + self.rz[0, j - 1].astype(F32)
+        if j > 1:
+            self.copy(2, 0, j - 2).wait_recv()
+            sum_a = sum_a + self.rz[0, j - 2].astype(F32)
         self.sz[0, j] = sum_a.astype(BF16)
         self.start(2, 0, j)
-        if j > 0:
-            self.copy(2, 1, j - 1).wait_recv()
-            sum_b = sum_b + self.rz[1, j - 1].astype(F32)
+        if j > 1:
+            self.copy(2, 1, j - 2).wait_recv()
+            sum_b = sum_b + self.rz[1, j - 2].astype(F32)
         if j < HALF - 1:
             self.sz[1, j] = sum_b.astype(BF16)
             self.start(2, 1, j)
@@ -197,8 +201,9 @@
             self.third(i - 2 * LAG)
 
     def finish(self):
-        self.copy(2, 0, HALF - 1).wait_recv()
-        self.kept[...] = self.kept[...] + self.rz[0, HALF - 1].astype(F32)
+        for d, j in ((0, HALF - 2), (1, HALF - 2), (0, HALF - 1)):
+            self.copy(2, d, j).wait_recv()
+            self.kept[...] = self.kept[...] + self.rz[d, j].astype(F32)
         for one in self.sent:
             one.wait_send()
 
@@ -237,7 +242,7 @@
         self.sent = []
 
     def copy(self, d, j):
-        to = self.place.along_z(1 if d == 0 else -1)
+        to = self.place.along_z(leap(d, j) if d == 0 else -leap(d, j))
         return remote(self.out.at[d, j], self.into.at[d, j], self.send.at[d, j], self.recv.at[d, j], to)
 
     def own(self, zz):
@@ -249,9 +254,9 @@
         far = (up_to(z + HALF - j, NZ), up_to(z + NZ - (HALF - 1 - j), NZ))
         for d in range(2):
             value = self.own(far[d])
-            if j > 0:
-                self.copy(d, j - 1).wait_recv()
-                value = value + self.into[d, j - 1].astype(F32)
+            if j > 1:
+                self.copy(d, j - 2).wait_recv()
+                value = value + self.into[d, j - 2].astype(F32)
             if d == 1 and j == HALF - 1:
                 self.kept[...] = value
             else:
@@ -261,8 +266,9 @@
                 self.sent.append(one)
 
     def finish(self):
-        self.copy(0, HALF - 1).wait_recv()
-        self.kept[...] = self.kept[...] + self.into[0, HALF - 1].astype(F32)
+        for d, j in ((0, HALF - 2), (1, HALF - 2), (0, HALF - 1)):
+            self.copy(d, j).wait_recv()
+            self.kept[...] = self.kept[...] + self.into[d, j].astype(F32)
         for one in self.sent:
             one.wait_send()
 
@@ -286,10 +292,11 @@
 
     def zcopy(self, what, d, j, received):
         z = self.place.z
-        back = j + 1 if received else j
+        step = min(2, j + 1)
+        back = j + 1 if received else j + 1 - step
         zz = up_to(z + NZ - back, NZ) if d == 0 else up_to(z + back, NZ)
         ref = self.rows.at[self.at(zz, 0), what]
-        to = self.place.along_z(1 if d == 0 else -1)
+        to = self.place.along_z(step if d == 0 else -step)
         return remote(ref, ref, self.zsend.at[what, d, j], self.zrecv.at[what, d, j], to)
 
     def ycopy(self, hop, d, q, received):
@@ -328,13 +335,14 @@
     def along_z(self, what, j):
         for d in self.hops(j):
             self.zcopy(what, d, j, True).wait_recv()
-            if d in self.hops(j + 1) and j + 1 < HALF:
-                self.start(self.zcopy(what, d, j + 1, False))
+            if j + 2 < HALF - d:
+                self.start(self.zcopy(what, d, j + 2, False))
         return [1 + 2 * j + d for d in self.hops(j)]
 
     def begin(self, what):
-        for d in range(2):
-            self.start(self.zcopy(what, d, 0, False))
+        for j in range(2):
+            for d in range(2):
+                self.start(self.zcopy(what, d, j, False))
 
     def run(self, collect):
         self.begin(0)
@@ -490,7 +498,7 @@
     barrier = pltpu.get_barrier_semaphore()
     near = [place.partner()]
     for d in (1, -1):
-        near += [place.along_x(d), place.along_y(d), place.along_z(d)]
+        near += [place.along_x(d), place.along_y(d), place.along_z(d), place.along_z(2 * d)]
     for device in near:
         pl.semaphore_signal(barrier, inc=1, device_id=device, device_id_type=MESH)
 
@@ -595,8 +603,10 @@
             block = slice(b * 16, (b + 1) * 16)
             grad = collect.grad(s, b)
             first, second = moments(exact_ref[0, s, block, :], exact_ref[1, s, block, :], grad)
-            first_ref[s, block, :] = first
-            second_ref[s, block, :] = second
+            for r in range(16):
+                lanes = slice((b * 16 + r) * TB, (b * 16 + r + 1) * TB)
+                first_ref[s : s + 1, lanes] = first[r : r + 1, :]
+                second_ref[s : s + 1, lanes] = second[r : r + 1, :]
 
 
 def body(
@@ -643,8 +653,8 @@
         kernel,
         out_shape=(
             jax.ShapeDtypeStruct((TILES * TB, TB), BF16),
-            jax.ShapeDtypeStruct((CAP, TB, TB), F32),
-            jax.ShapeDtypeStruct((CAP, TB, TB), F32),
+            jax.ShapeDtypeStruct((CAP, TB * TB), F32),
+            jax.ShapeDtypeStruct((CAP, TB * TB), F32),
         ),
         in_specs=[smem] * 2 + [vmem] * 7,
         out_specs=[vmem] * 3,

time: 138 us -> 114 us (0.83)
  the two profiles are of different devices: /device:TPU:8 before, /device:TPU:6 now
where the time goes in v3:
time: 114 us
  Pallas kernels  107 us (94%)
  local copies, waits for them, and re-layouts  5.99 us (5%)
    pallas_call x1, Pallas kernels, body(): pl.pallas_call(kernel, out_shape=(jax.ShapeDtypeStruct((TILES * TB, TB),...  105 us
    unnamed x7, local copies, waits for them, and re-layouts  4.3 us

profile of v3, /device:TPU:6, one launch (start us, length us, event | category | flops | bytes accessed | tf_op | source)
XLA Modules:
  0.0 113.9 jit_solution(7937435431505787313)
XLA Ops:
  0.6 1.7 %copy_bitcast_fusion = (s32[2,128,128]{2,1,0:T(8,128)}, s32[2,128,128]{2,1,0:T(8,128)}) fusion(s32[1,2,128,128]{3,1,2,0:T(2,128)} %bitcast.19, s32[1,2,128,128]{3,1,2,0:T(2,128)} %bitcast.20), kind=kLoop, calls=%fused_computation | loop fusion | bytes 524288 | tf_op jit(solution)/shard_map/reshape | solution.py:647
  2.3 2.1 %shard_map.148 = (f32[2,2,128,128]{3,2,1,0:T(8,128)}, bf16[2,2,128,128]{3,2,1,0:T(8,128)(2,1)}) custom-call(f32[2,8]{1,0:T(2,128)} %bitcast.22, f32[2,8]{1,0:T(2,128)} %bitcast.23, s32[2,128,128]{2,1,0:T(8,128)} %get-tuple-element.14.fcodes, s32[2,128,128]{2,1,0:T(8,128)} %get-tuple-element.13.scodes, f32[2,128]{1,0:T(2,128)} %bitcast.24, f32[2,128]{1,0:T(2,128)} %bitcast.25), custom_call_target="tpu_custom_call" | custom-call | tf_op jit(solution)/shard_map/pallas_call | solution.py:635
  4.4 105.2 %shard_map.149 = (bf16[7168,128]{1,0:T(8,128)(2,1)}, f32[2,16384]{1,0:T(2,128)}, f32[2,16384]{1,0:T(2,128)}) custom-call(s32[3,56]{1,0:T(4,128)} %bitcast.21, s32[56]{0:T(128)} %slots_ref.1, f32[2,2,128,128]{3,2,1,0:T(8,128)} %get-tuple-element.8.exact_ref, bf16[2,2,128,128]{3,2,1,0:T(8,128)(2,1)} %get-tuple-element.9.rounded_ref, ...), custom_call_target="tpu_custom_call" | custom-call | tf_op jit(solution)/shard_map/pallas_call | solution.py:652
  109.6 0.0 copy-start.1
  109.6 0.0 copy-start
  109.6 3.0 %copy.23 = bf16[56,128,128]{2,1,0:T(8,128)(2,1)} copy(bf16[56,128,128]{2,1,0:T(8,128)(2,1)} %bitcast.16) | data formatting | bytes 3670016
  112.6 0.0 copy-done.1
  112.6 0.7 copy.24
  113.3 0.0 copy-done
  113.3 0.7 copy.25
Async XLA Ops:
  109.6 3.0 %copy-start.1 = (f32[2,16384]{1,0:T(2,128)S(1)}, f32[2,16384]{1,0:T(2,128)}, u32[]{:S(2)}) copy-start(f32[2,16384]{1,0:T(2,128)} %get-tuple-element.11) | copy-start | bytes 393220
  109.6 3.7 %copy-start = (f32[2,16384]{1,0:T(2,128)S(1)}, f32[2,16384]{1,0:T(2,128)}, u32[]{:S(2)}) copy-start(f32[2,16384]{1,0:T(2,128)} %get-tuple-element.12) | copy-start | bytes 393220

commit v4 on v3

--- a/solution.py
+++ b/solution.py
@@ -23,6 +23,7 @@
 ROWS = TILES * TB // (NY * NZ)
 HALF = NZ // 2
 LAG = 2
+EARLY = 4
 MESH = pl.DeviceIdType.MESH
 F32, BF16 = jnp.float32, jnp.bfloat16
 
@@ -55,6 +56,12 @@
     return pltpu.make_async_remote_copy(
         src_ref=src, dst_ref=dst, send_sem=send, recv_sem=recv, device_id=device, device_id_type=MESH
     )
+
+
+def moments(first_old, second_old, grad):
+    first = BETA_FIRST * first_old + (1.0 - BETA_FIRST) * grad
+    second = BETA_SECOND * second_old + (1.0 - BETA_SECOND) * grad * grad
+    return first, second
 
 
 def leap(d, j):
@@ -129,7 +136,8 @@
 
 
 class Scatter:
-    def __init__(self, place, source, bufs, send, recv, kept):
+    def __init__(self, place, source, bufs, send, recv, kept, make):
+        self.make = make
         self.place, self.source, self.send, self.recv, self.kept = place, source, send, recv, kept
         self.s1, self.r1, self.s2, self.r2, self.sz, self.rz = bufs
         self.sent = []
@@ -156,6 +164,8 @@
 
     def first(self, j):
         za, zb = self.zs(j)
+        self.make(za)
+        self.make(zb)
         self.s1[0, j] = self.own(za, 2)
         self.start(0, 0, j)
         self.s1[1, j] = self.own(zb, 2)
@@ -433,7 +443,7 @@
         for s in range(CAP):
             for b in range(TB * TB // QB):
                 block = slice(b * 16, (b + 1) * 16)
-                code = codes[s, block, :]
+                code = codes[block, s, :]
                 low = jnp.bitwise_and(code, TB - 1)
                 value = jnp.where(
                     code < TB,
@@ -448,7 +458,6 @@
 def kernel(
     list_ref,
     slots_ref,
-    exact_ref,
     rounded_ref,
     input_ref,
     grad_ref,
@@ -456,8 +465,7 @@
     up_ref,
     hgrad_ref,
     update_ref,
-    first_ref,
-    second_ref,
+    grad_out_ref,
     left,
     right,
     parts,
@@ -493,6 +501,7 @@
     yrecv,
     csend,
     crecv,
+    out_sem,
 ):
     place = Place()
     barrier = pltpu.get_barrier_semaphore()
@@ -545,7 +554,8 @@
     shared.finish()
     lax.fori_loop(0, TILES, fill, 0)
     for i in range(HALF):
-        olds.slot(i)
+        if i < EARLY:
+            olds.slot(i)
         gather.step(i + 1)
         if i + 2 < HB // 4:
             activations(i + 2)
@@ -559,7 +569,6 @@
     ]
     tiles = lax.fori_loop(0, TILES, find, (jnp.int32(TILES),) * len(wanted))
     summed[...] = jnp.zeros(summed.shape, BF16)
-    olds.finish()
     gather.finish()
 
     def multiply(k, carry):
@@ -570,17 +579,17 @@
         parts[0, pl.ds(pl.multiple_of(k * TB, TB), TB), :] = tile.astype(BF16)
         return carry
 
-    lax.fori_loop(0, TILES, multiply, 0, unroll=4)
-
-    sums = Scatter(place, parts, (p1, q1, p2, q2, pz, qz), psend, precv, sum_kept)
+    def products(zz):
+        start = NY * ROWS * zz // TB
+        lax.fori_loop(0, NY * ROWS // TB + 1, lambda i, carry: multiply(start + i, carry), 0, unroll=True)
+
+    sums = Scatter(place, parts, (p1, q1, p2, q2, pz, qz), psend, precv, sum_kept, products)
     for i in range(HALF + 2 * LAG):
         sums.slot(i)
+        if i + EARLY < HALF:
+            olds.slot(i + EARLY)
+    olds.finish()
     sums.finish()
-
-    def moments(first_old, second_old, grad):
-        first = BETA_FIRST * first_old + (1.0 - BETA_FIRST) * grad
-        second = BETA_SECOND * second_old + (1.0 - BETA_SECOND) * grad * grad
-        return first, second
 
     grad = sum_kept[0]
     first, second = moments(old_kept[0], old_kept[1], grad)
@@ -589,8 +598,13 @@
     rows[place.dp, 0] = (first_hat / (jnp.sqrt(second_hat) + EPSILON)).astype(BF16)
     rows[place.dp, 1] = grad.astype(BF16)
 
+    gives = []
+
     def give(dp):
-        update_ref[pl.ds(pl.multiple_of(dp * ROWS, 16), ROWS), :] = rows[dp, 0]
+        where = pl.ds(pl.multiple_of(dp * ROWS, 16), ROWS)
+        one = pltpu.make_async_copy(rows.at[dp, 0], update_ref.at[where], out_sem.at[len(gives)])
+        one.start()
+        gives.append(one)
 
     def take(dp):
         summed[pl.ds(dp * (ROWS // 16), ROWS // 16)] = rows[dp, 1].reshape(ROWS // 16, 16, TB)
@@ -600,13 +614,31 @@
     collect.finish()
     for s in range(CAP):
         for b in range(8):
-            block = slice(b * 16, (b + 1) * 16)
-            grad = collect.grad(s, b)
-            first, second = moments(exact_ref[0, s, block, :], exact_ref[1, s, block, :], grad)
-            for r in range(16):
-                lanes = slice((b * 16 + r) * TB, (b * 16 + r + 1) * TB)
-                first_ref[s : s + 1, lanes] = first[r : r + 1, :]
-                second_ref[s : s + 1, lanes] = second[r : r + 1, :]
+            grad_out_ref[s, b * 16 : (b + 1) * 16, :] = collect.grad(s, b)
+    for one in gives:
+        one.wait()
+
+
+def finish(update_ref, grad_ref, exact_ref, out_ref, first_ref, second_ref, buffer, into, out):
+    count = into.shape[0]
+    size = TILES * TB // count
+    copies = []
+    for i in range(count):
+        where = pl.ds(i * size, size)
+        one = pltpu.make_async_copy(update_ref.at[where], buffer.at[where], into.at[i])
+        one.start()
+        copies.append((one, pltpu.make_async_copy(buffer.at[where], out_ref.at[where], out.at[i])))
+    for one, two in copies:
+        one.wait()
+        two.start()
+    for s in range(CAP):
+        for b in range(16):
+            block = slice(b * 8, (b + 1) * 8)
+            first, second = moments(exact_ref[0, s, block, :], exact_ref[1, s, block, :], grad_ref[s, block, :])
+            first_ref[block, s, :] = first
+            second_ref[block, s, :] = second
+    for one, two in copies:
+        two.wait()
 
 
 def body(
@@ -643,21 +675,20 @@
     )(
         first_absmax[0],
         second_absmax[0],
-        first_codes.reshape(CAP, TB, TB),
-        second_codes.reshape(CAP, TB, TB),
+        first_codes.reshape(CAP, TB, TB).transpose(1, 0, 2),
+        second_codes.reshape(CAP, TB, TB).transpose(1, 0, 2),
         signed_map.reshape(2, TB),
         unsigned_map.reshape(2, TB),
     )
     dma = pltpu.SemaphoreType.DMA
-    update, first, second = pl.pallas_call(
+    update, grad = pl.pallas_call(
         kernel,
         out_shape=(
             jax.ShapeDtypeStruct((TILES * TB, TB), BF16),
-            jax.ShapeDtypeStruct((CAP, TB * TB), F32),
-            jax.ShapeDtypeStruct((CAP, TB * TB), F32),
+            jax.ShapeDtypeStruct((CAP, TB, TB), F32),
         ),
-        in_specs=[smem] * 2 + [vmem] * 7,
-        out_specs=[vmem] * 3,
+        in_specs=[smem] * 2 + [vmem] * 6,
+        out_specs=[pl.BlockSpec(memory_space=pl.ANY), vmem],
         scratch_shapes=[
             pltpu.VMEM((WB + HB, TB, TB), BF16),
             pltpu.VMEM((WB + 2 * HB, TB, TB), BF16),
@@ -683,14 +714,14 @@
         + [dma((3, 2, HALF))] * 2
         + [dma((2, 2, HALF))] * 2
         + [dma((2, 2, NZ))] * 2
-        + [dma((3, 2))] * 2,
+        + [dma((3, 2))] * 2
+        + [dma((NY * NZ,))],
         compiler_params=pltpu.CompilerParams(
             collective_id=0, has_side_effects=True, vmem_limit_bytes=60 * 1024 * 1024
         ),
     )(
         tile_list.T,
         tile_slots,
-        exact,
         rounded,
         layer_input,
         output_grad,
@@ -698,10 +729,22 @@
         up_pre,
         hidden_grad,
     )
+    anywhere = pl.BlockSpec(memory_space=pl.ANY)
+    update, first, second = pl.pallas_call(
+        finish,
+        out_shape=(
+            jax.ShapeDtypeStruct((TILES * TB, TB), BF16),
+            jax.ShapeDtypeStruct((TB, CAP, TB), F32),
+            jax.ShapeDtypeStruct((TB, CAP, TB), F32),
+        ),
+        in_specs=[anywhere, vmem, vmem],
+        out_specs=[anywhere, vmem, vmem],
+        scratch_shapes=[pltpu.VMEM((TILES * TB, TB), BF16), dma((8,)), dma((8,))],
+    )(update, grad, exact)
     return (
         update.reshape(TILES, TB, TB),
-        first.reshape(1, CAP, TB * TB),
-        second.reshape(1, CAP, TB * TB),
+        first.transpose(1, 0, 2).reshape(1, CAP, TB * TB),
+        second.transpose(1, 0, 2).reshape(1, CAP, TB * TB),
     )
 
 

time: 114 us -> 104 us (0.912)
  the two profiles are of different devices: /device:TPU:6 before, /device:TPU:10 now
where the time goes in v4:
time: 104 us
  Pallas kernels  103 us (99%)
    pallas_call x1, Pallas kernels, body(): pl.pallas_call(kernel, out_shape=(jax.ShapeDtypeStruct((TILES * TB, TB),...  96.4 us
    pallas_call x1, Pallas kernels, body(): pl.pallas_call(finish, out_shape=(jax.ShapeDtypeStruct((TILES * TB, TB),...  4.13 us
    pallas_call x1, Pallas kernels, body(): pl.pallas_call(dequantize, out_shape=(jax.ShapeDtypeStruct((2, CAP, TB, T...  2.41 us

profile of v4, /device:TPU:10, one launch (start us, length us, event | category | flops | bytes accessed | tf_op | source)
XLA Modules:
  0.0 103.6 jit_solution(3780398960361105104)
XLA Ops:
  0.6 2.4 %shard_map.148 = (f32[2,2,128,128]{3,2,1,0:T(8,128)}, bf16[2,2,128,128]{3,2,1,0:T(8,128)(2,1)}) custom-call(f32[2,8]{1,0:T(2,128)} %bitcast.21, f32[2,8]{1,0:T(2,128)} %bitcast.22, s32[128,2,128]{2,1,0:T(2,128)} %bitcast.18, s32[128,2,128]{2,1,0:T(2,128)} %bitcast.19, f32[2,128]{1,0:T(2,128)} %bitcast.23, f32[2,128]{1,0:T(2,128)} %bitcast.24), custom_call_target="tpu_custom_call" | custom-call | tf_op jit(solution)/shard_map/pallas_call | solution.py:667
  3.0 96.4 %shard_map.149 = (bf16[7168,128]{1,0:T(8,128)(2,1)}, f32[2,128,128]{2,1,0:T(8,128)}) custom-call(s32[3,56]{1,0:T(4,128)} %bitcast.20, s32[56]{0:T(128)} %slots_ref.1, bf16[2,2,128,128]{3,2,1,0:T(8,128)(2,1)} %get-tuple-element.10.rounded_ref, bf16[128,1024]{1,0:T(8,128)(2,1)} %input_ref.1, bf16[128,1024]{1,0:T(8,128)(2,1)} %grad_ref.1, ...), custom_call_target="tpu_custom_call" | custom-call | tf_op jit(solution)/shard_map/pallas_call | solution.py:684
  99.5 4.1 %shard_map.150 = (bf16[7168,128]{1,0:T(8,128)(2,1)}, f32[128,2,128]{2,1,0:T(2,128)}, f32[128,2,128]{2,1,0:T(2,128)}) custom-call(bf16[7168,128]{1,0:T(8,128)(2,1)} %get-tuple-element.11.update_ref, f32[2,128,128]{2,1,0:T(8,128)} %get-tuple-element.12.grad_ref, f32[2,2,128,128]{3,2,1,0:T(8,128)} %get-tuple-element.13.exact_ref), custom_call_target="tpu_custom_call" | custom-call | tf_op jit(solution)/shard_map/pallas_call | solution.py:733

commit v5 on v4

--- a/solution.py
+++ b/solution.py
@@ -131,8 +131,6 @@
         for p in range(4):
             for route in (2, 3, 4, 6):
                 self.arrived(route, p)
-        for one in self.sent:
-            one.wait_send()
 
 
 class Scatter:
@@ -214,8 +212,6 @@
         for d, j in ((0, HALF - 2), (1, HALF - 2), (0, HALF - 1)):
             self.copy(2, d, j).wait_recv()
             self.kept[...] = self.kept[...] + self.rz[d, j].astype(F32)
-        for one in self.sent:
-            one.wait_send()
 
 
 class Pool:
@@ -241,8 +237,6 @@
     def finish(self):
         for d in range(2):
             self.copy(1, d, True).wait_recv()
-        for one in self.sent:
-            one.wait_send()
 
 
 class Olds:
@@ -279,8 +273,6 @@
         for d, j in ((0, HALF - 2), (1, HALF - 2), (0, HALF - 1)):
             self.copy(d, j).wait_recv()
             self.kept[...] = self.kept[...] + self.into[d, j].astype(F32)
-        for one in self.sent:
-            one.wait_send()
 
 
 class Spread:
@@ -355,32 +347,27 @@
                 self.start(self.zcopy(what, d, j, False))
 
     def run(self, collect):
-        self.begin(0)
-        self.begin(1)
         self.out_y(0)
         self.take(self.at(self.place.z, 0))
         groups = [[0]]
         for j in range(HALF + 4):
             if j < HALF:
+                for q in self.along_z(1, j):
+                    self.take(self.at(self.zq(q), 0))
+                if j == HALF - 1:
+                    collect.first()
                 group = self.along_z(0, j)
                 for q in group:
                     self.out_y(q)
                 groups.append(group)
-            if 0 < j <= HALF:
-                for q in self.along_z(1, j - 1):
-                    self.take(self.at(self.zq(q), 0))
-            if j == HALF:
-                collect.first()
             if j < len(groups):
                 for q in groups[j]:
                     self.on_y(q)
-            if j == HALF + 1:
+            if j == HALF - 1:
                 collect.second()
             if 0 <= j - 2 < len(groups):
                 for q in groups[j - 2]:
                     self.done(q)
-        for one in self.sent:
-            one.wait_send()
 
 
 class Collect:
@@ -425,8 +412,6 @@
         for hop in (0, 2):
             for d in range(2):
                 self.copy(hop, d).wait_recv()
-        for one in self.sent:
-            one.wait_send()
 
     def grad(self, s, b):
         block = slice(b * 16, (b + 1) * 16)
@@ -461,9 +446,9 @@
     rounded_ref,
     input_ref,
     grad_ref,
-    gate_ref,
-    up_ref,
-    hgrad_ref,
+    gate_hbm,
+    up_hbm,
+    hgrad_hbm,
     update_ref,
     grad_out_ref,
     left,
@@ -502,8 +487,18 @@
     csend,
     crecv,
     out_sem,
+    load_sem,
+    gate_ref,
+    up_ref,
+    hgrad_ref,
 ):
     place = Place()
+    loads = [
+        pltpu.make_async_copy(src, dst, load_sem.at[i])
+        for i, (src, dst) in enumerate(((gate_hbm, gate_ref), (up_hbm, up_ref), (hgrad_hbm, hgrad_ref)))
+    ]
+    for one in loads:
+        one.start()
     barrier = pltpu.get_barrier_semaphore()
     near = [place.partner()]
     for d in (1, -1):
@@ -547,6 +542,8 @@
         return carry
 
     olds = Olds(place, states, oz, iz, esend, erecv, old_kept)
+    for one in loads:
+        one.wait()
     activations(0)
     shared.start(1)
     activations(1)
@@ -591,54 +588,78 @@
     olds.finish()
     sums.finish()
 
+    gives = []
+
+    def give(dp):
+        where = pl.ds(pl.multiple_of(dp * ROWS, 16), ROWS)
+        one = pltpu.make_async_copy(rows.at[dp, 0], update_ref.at[where], out_sem.at[len(gives)])
+        one.start()
+        gives.append(one)
+
+    def take(dp):
+        summed[pl.ds(dp * (ROWS // 16), ROWS // 16)] = rows[dp, 1].reshape(ROWS // 16, 16, TB)
+
+    collect = Collect(place, tiles, summed, cout, cinto, crelay, clast, csend, crecv)
+    spread = Spread(place, rows, zsend, zrecv, ysend, yrecv, give, take)
     grad = sum_kept[0]
+    rows[place.dp, 1] = grad.astype(BF16)
+    spread.begin(1)
     first, second = moments(old_kept[0], old_kept[1], grad)
     first_hat = first / (1.0 - BETA_FIRST**STEP)
     second_hat = second / (1.0 - BETA_SECOND**STEP)
     rows[place.dp, 0] = (first_hat / (jnp.sqrt(second_hat) + EPSILON)).astype(BF16)
-    rows[place.dp, 1] = grad.astype(BF16)
-
-    gives = []
-
-    def give(dp):
-        where = pl.ds(pl.multiple_of(dp * ROWS, 16), ROWS)
-        one = pltpu.make_async_copy(rows.at[dp, 0], update_ref.at[where], out_sem.at[len(gives)])
-        one.start()
-        gives.append(one)
-
-    def take(dp):
-        summed[pl.ds(dp * (ROWS // 16), ROWS // 16)] = rows[dp, 1].reshape(ROWS // 16, 16, TB)
-
-    collect = Collect(place, tiles, summed, cout, cinto, crelay, clast, csend, crecv)
-    Spread(place, rows, zsend, zrecv, ysend, yrecv, give, take).run(collect)
+    spread.begin(0)
+    spread.run(collect)
     collect.finish()
     for s in range(CAP):
         for b in range(8):
             grad_out_ref[s, b * 16 : (b + 1) * 16, :] = collect.grad(s, b)
+    for phase in (shared, gather, olds, sums, spread, collect):
+        for one in phase.sent:
+            one.wait_send()
     for one in gives:
         one.wait()
 
 
-def finish(update_ref, grad_ref, exact_ref, out_ref, first_ref, second_ref, buffer, into, out):
+def finish(
+    update_hbm, grad_hbm, exact_hbm, out_ref, first_out, second_out, buffer, grad_ref, exact_ref, first_ref, second_ref,
+    into, out, extra,
+):
     count = into.shape[0]
     size = TILES * TB // count
+    loads = [
+        pltpu.make_async_copy(exact_hbm, exact_ref, extra.at[0]),
+        pltpu.make_async_copy(grad_hbm, grad_ref, extra.at[1]),
+    ]
+    for one in loads:
+        one.start()
     copies = []
     for i in range(count):
         where = pl.ds(i * size, size)
-        one = pltpu.make_async_copy(update_ref.at[where], buffer.at[where], into.at[i])
+        one = pltpu.make_async_copy(update_hbm.at[where], buffer.at[where], into.at[i])
         one.start()
         copies.append((one, pltpu.make_async_copy(buffer.at[where], out_ref.at[where], out.at[i])))
-    for one, two in copies:
+    for one in loads:
         one.wait()
-        two.start()
     for s in range(CAP):
-        for b in range(16):
-            block = slice(b * 8, (b + 1) * 8)
+        for b in range(8):
+            block = slice(b * 16, (b + 1) * 16)
             first, second = moments(exact_ref[0, s, block, :], exact_ref[1, s, block, :], grad_ref[s, block, :])
             first_ref[block, s, :] = first
             second_ref[block, s, :] = second
+            if s == 0:
+                copies[b][0].wait()
+                copies[b][1].start()
+    stores = [
+        pltpu.make_async_copy(first_ref, first_out, extra.at[2]),
+        pltpu.make_async_copy(second_ref, second_out, extra.at[3]),
+    ]
+    for one in stores:
+        one.start()
     for one, two in copies:
         two.wait()
+    for one in stores:
+        one.wait()
 
 
 def body(
@@ -658,6 +679,7 @@
 ):
     vmem = pl.BlockSpec(memory_space=pltpu.VMEM)
     smem = pl.BlockSpec(memory_space=pltpu.SMEM)
+    anywhere = pl.BlockSpec(memory_space=pl.ANY)
 
     def scatter_shapes(n):
         one = [pltpu.VMEM((2, HALF, n, ROWS, TB), BF16)] * 2
@@ -687,8 +709,8 @@
             jax.ShapeDtypeStruct((TILES * TB, TB), BF16),
             jax.ShapeDtypeStruct((CAP, TB, TB), F32),
         ),
-        in_specs=[smem] * 2 + [vmem] * 6,
-        out_specs=[pl.BlockSpec(memory_space=pl.ANY), vmem],
+        in_specs=[smem] * 2 + [vmem] * 3 + [anywhere] * 3,
+        out_specs=[anywhere, vmem],
         scratch_shapes=[
             pltpu.VMEM((WB + HB, TB, TB), BF16),
             pltpu.VMEM((WB + 2 * HB, TB, TB), BF16),
@@ -715,7 +737,8 @@
         + [dma((2, 2, HALF))] * 2
         + [dma((2, 2, NZ))] * 2
         + [dma((3, 2))] * 2
-        + [dma((NY * NZ,))],
+        + [dma((NY * NZ,)), dma((3,))]
+        + [pltpu.VMEM(gate_pre.shape, BF16)] * 3,
         compiler_params=pltpu.CompilerParams(
             collective_id=0, has_side_effects=True, vmem_limit_bytes=60 * 1024 * 1024
         ),
@@ -729,7 +752,6 @@
         up_pre,
         hidden_grad,
     )
-    anywhere = pl.BlockSpec(memory_space=pl.ANY)
     update, first, second = pl.pallas_call(
         finish,
         out_shape=(
@@ -737,9 +759,18 @@
             jax.ShapeDtypeStruct((TB, CAP, TB), F32),
             jax.ShapeDtypeStruct((TB, CAP, TB), F32),
         ),
-        in_specs=[anywhere, vmem, vmem],
-        out_specs=[anywhere, vmem, vmem],
-        scratch_shapes=[pltpu.VMEM((TILES * TB, TB), BF16), dma((8,)), dma((8,))],
+        in_specs=[anywhere] * 3,
+        out_specs=[anywhere] * 3,
+        scratch_shapes=[
+            pltpu.VMEM((TILES * TB, TB), BF16),
+            pltpu.VMEM((CAP, TB, TB), F32),
+            pltpu.VMEM((2, CAP, TB, TB), F32),
+            pltpu.VMEM((TB, CAP, TB), F32),
+            pltpu.VMEM((TB, CAP, TB), F32),
+            dma((8,)),
+            dma((8,)),
+            dma((4,)),
+        ],
     )(update, grad, exact)
     return (
         update.reshape(TILES, TB, TB),

time: 104 us -> 103 us (level)
  the two profiles are of different devices: /device:TPU:10 before, /device:TPU:6 now
where the time goes in v5:
time: 103 us; the launch traced here: 102 us
  Pallas kernels  102 us (99%)
    pallas_call x1, Pallas kernels, body(): pl.pallas_call(kernel, out_shape=(jax.ShapeDtypeStruct((TILES * TB, TB),...  96.3 us
    pallas_call x1, Pallas kernels, body(): pl.pallas_call(finish, out_shape=(jax.ShapeDtypeStruct((TILES * TB, TB),...  3.09 us
    pallas_call x1, Pallas kernels, body(): pl.pallas_call(dequantize, out_shape=(jax.ShapeDtypeStruct((2, CAP, TB, T...  2.41 us

profile of v5, /device:TPU:6, one launch (start us, length us, event | category | flops | bytes accessed | tf_op | source)
XLA Modules:
  0.0 102.5 jit_solution(16449878727584754445)
XLA Ops:
  0.6 2.4 %shard_map.148 = (f32[2,2,128,128]{3,2,1,0:T(8,128)}, bf16[2,2,128,128]{3,2,1,0:T(8,128)(2,1)}) custom-call(f32[2,8]{1,0:T(2,128)} %bitcast.21, f32[2,8]{1,0:T(2,128)} %bitcast.22, s32[128,2,128]{2,1,0:T(2,128)} %bitcast.18, s32[128,2,128]{2,1,0:T(2,128)} %bitcast.19, f32[2,128]{1,0:T(2,128)} %bitcast.23, f32[2,128]{1,0:T(2,128)} %bitcast.24), custom_call_target="tpu_custom_call" | custom-call | tf_op jit(solution)/shard_map/pallas_call | solution.py:689
  3.0 96.3 %shard_map.149 = (bf16[7168,128]{1,0:T(8,128)(2,1)}, f32[2,128,128]{2,1,0:T(8,128)}) custom-call(s32[3,56]{1,0:T(4,128)} %bitcast.20, s32[56]{0:T(128)} %slots_ref.1, bf16[2,2,128,128]{3,2,1,0:T(8,128)(2,1)} %get-tuple-element.10.rounded_ref, bf16[128,1024]{1,0:T(8,128)(2,1)} %input_ref.1, bf16[128,1024]{1,0:T(8,128)(2,1)} %grad_ref.1, ...), custom_call_target="tpu_custom_call" | custom-call | tf_op jit(solution)/shard_map/pallas_call | solution.py:706
  99.4 3.1 %shard_map.150 = (bf16[7168,128]{1,0:T(8,128)(2,1)}, f32[128,2,128]{2,1,0:T(2,128)}, f32[128,2,128]{2,1,0:T(2,128)}) custom-call(bf16[7168,128]{1,0:T(8,128)(2,1)} %get-tuple-element.11.update_hbm, f32[2,128,128]{2,1,0:T(8,128)} %get-tuple-element.12.grad_hbm, f32[2,2,128,128]{3,2,1,0:T(8,128)} %get-tuple-element.13.exact_hbm), custom_call_target="tpu_custom_call" | custom-call | tf_op jit(solution)/shard_map/pallas_call | solution.py:755

commit v6 on v5

--- a/solution.py
+++ b/solution.py
@@ -360,13 +360,13 @@
                 for q in group:
                     self.out_y(q)
                 groups.append(group)
-            if j < len(groups):
-                for q in groups[j]:
+            if j == HALF:
+                collect.second()
+            if 0 <= j - 1 < len(groups):
+                for q in groups[j - 1]:
                     self.on_y(q)
-            if j == HALF - 1:
-                collect.second()
-            if 0 <= j - 2 < len(groups):
-                for q in groups[j - 2]:
+            if 0 <= j - 3 < len(groups):
+                for q in groups[j - 3]:
                     self.done(q)
 
 

time: 103 us -> 101 us (0.981)
  Pallas kernels: 102 us -> 100 us
    pallas_call x1, Pallas kernels: 96.3 us -> 94.7 us  [body(): pl.pallas_call(kernel, out_shape=(jax.ShapeDtypeStruct((TILES * TB, TB),...]
where the time goes in v6:
time: 101 us
  Pallas kernels  100 us (99%)
    pallas_call x1, Pallas kernels, body(): pl.pallas_call(kernel, out_shape=(jax.ShapeDtypeStruct((TILES * TB, TB),...  94.7 us
    pallas_call x1, Pallas kernels, body(): pl.pallas_call(finish, out_shape=(jax.ShapeDtypeStruct((TILES * TB, TB),...  3.09 us
    pallas_call x1, Pallas kernels, body(): pl.pallas_call(dequantize, out_shape=(jax.ShapeDtypeStruct((2, CAP, TB, T...  2.41 us

profile of v6, /device:TPU:6, one launch (start us, length us, event | category | flops | bytes accessed | tf_op | source)
XLA Modules:
  0.0 100.8 jit_solution(7730859317311809142)
XLA Ops:
  0.6 2.4 %shard_map.148 = (f32[2,2,128,128]{3,2,1,0:T(8,128)}, bf16[2,2,128,128]{3,2,1,0:T(8,128)(2,1)}) custom-call(f32[2,8]{1,0:T(2,128)} %bitcast.21, f32[2,8]{1,0:T(2,128)} %bitcast.22, s32[128,2,128]{2,1,0:T(2,128)} %bitcast.18, s32[128,2,128]{2,1,0:T(2,128)} %bitcast.19, f32[2,128]{1,0:T(2,128)} %bitcast.23, f32[2,128]{1,0:T(2,128)} %bitcast.24), custom_call_target="tpu_custom_call" | custom-call | tf_op jit(solution)/shard_map/pallas_call | solution.py:689
  3.0 94.7 %shard_map.149 = (bf16[7168,128]{1,0:T(8,128)(2,1)}, f32[2,128,128]{2,1,0:T(8,128)}) custom-call(s32[3,56]{1,0:T(4,128)} %bitcast.20, s32[56]{0:T(128)} %slots_ref.1, bf16[2,2,128,128]{3,2,1,0:T(8,128)(2,1)} %get-tuple-element.10.rounded_ref, bf16[128,1024]{1,0:T(8,128)(2,1)} %input_ref.1, bf16[128,1024]{1,0:T(8,128)(2,1)} %grad_ref.1, ...), custom_call_target="tpu_custom_call" | custom-call | tf_op jit(solution)/shard_map/pallas_call | solution.py:706
  97.7 3.1 %shard_map.150 = (bf16[7168,128]{1,0:T(8,128)(2,1)}, f32[128,2,128]{2,1,0:T(2,128)}, f32[128,2,128]{2,1,0:T(2,128)}) custom-call(bf16[7168,128]{1,0:T(8,128)(2,1)} %get-tuple-element.11.update_hbm, f32[2,128,128]{2,1,0:T(8,128)} %get-tuple-element.12.grad_hbm, f32[2,2,128,128]{3,2,1,0:T(8,128)} %get-tuple-element.13.exact_hbm), custom_call_target="tpu_custom_call" | custom-call | tf_op jit(solution)/shard_map/pallas_call | solution.py:755
